TPU v7x, 32 devices: a whole 2x2x4 slice. The times are simulated.
32 devices in a mesh: wide: 4 (over y, core), narrow: 4 (over z), depth: 2 (over x).
Axes of the slice: x: 2, y: 2, z: 4, core: 2. Of those that a mesh axis runs over, the one named last changes fastest.
Arguments:
- hidden_state: bfloat16 [16, 4096], P(('wide', 'depth')), may hold values from -6 to 6
- query_weight: bfloat16 [4096, 4096], P('depth', 'narrow'), may hold values from -0.09375 to 0.09375
- output_weight: bfloat16 [4096, 4096], P('narrow'), may hold values from -0.09375 to 0.09375
- cache_keys: bfloat16 [16, 512, 4096], P(('wide', 'depth'), None, 'narrow'), may hold values from -128 to 128
- cache_values: bfloat16 [16, 512, 4096], P(('wide', 'depth'), None, 'narrow'), may hold values from -12 to 12
- enc_blocks: int32 [16], replicated, may hold values from 1 to 4
- cache_slot: int32 [16], replicated, may hold values from 0 to 15, as said below
Outputs:
- attended: bfloat16 [16, 4096], P(('wide', 'depth'), 'narrow')
Inputs may be any that keep to these rules, and one draw needn't show every extreme that they name: Request r attends to the first 128 * enc_blocks[r] rows of its cache slot. Every slot holds exactly one request, and r and cache_slot[r] agree in their value of (index // 2) % 2.
All inputs are finite; a program needn't handle non-finite values.
Results may differ from a plain program's by a relative error of at most 0.012.
The roundings to bfloat16 on the way count: a program that leaves them out, or rounds other values in their place, can miss the bound.
Values may be sent and summed in bfloat16 or wider, within the bound.
No kernel may reach another device: no remote copies, remote signals or barrier semaphores. Data moves between devices by JAX's collectives and lax.ppermute only.
A program may use at most 64 MiB of HBM per device.

v0:
```python
import jax
import jax.numpy as jnp
from jax import lax
from jax.sharding import PartitionSpec as P

HDIM = 64
BLOCK = 128


def attend_pairs(queries, key_rows, value_rows, chosen, block_count):
    query_count = queries.shape[0]
    piece_rows, cache_len, features = key_rows.shape
    head_count = features // HDIM
    query_heads = queries.reshape(query_count, head_count, HDIM)
    key_heads = key_rows.reshape(piece_rows, cache_len, head_count, HDIM)
    value_heads = value_rows.reshape(piece_rows, cache_len, head_count, HDIM)
    scores = jnp.einsum(
        "ahd,blhd->abhl", query_heads, key_heads, preferred_element_type=jnp.float32
    )
    usable = jnp.arange(cache_len, dtype=jnp.int32)[None, :] < (block_count * BLOCK)[:, None]
    scores = jnp.where(usable[:, None, None, :], scores, jnp.float32(-1e30))
    row_top = jnp.max(scores, axis=-1, keepdims=True)
    raised = jnp.exp(scores - row_top)
    shares = (raised / jnp.sum(raised, axis=-1, keepdims=True)).astype(jnp.bfloat16)
    shares = shares * chosen[:, :, None, None]
    context = jnp.einsum("abhl,blhd->ahd", shares, value_heads, preferred_element_type=jnp.float32)
    return context.reshape(query_count, features)


def shards(
    hidden_state, query_weight, output_weight, cache_keys, cache_values, enc_blocks, cache_slot
):
    row_count = hidden_state.shape[0]
    halves = lax.axis_size("depth")
    at_depth = lax.axis_index("depth")
    at_wide = lax.axis_index("wide")
    widened = hidden_state.astype(jnp.float32)
    mean_square = jnp.mean(widened * widened, axis=-1, keepdims=True)
    normed = (widened * lax.rsqrt(mean_square + 1e-06)).astype(jnp.bfloat16)
    col_width = query_weight.shape[0]
    columns = lax.dynamic_slice_in_dim(
        lax.all_gather(normed, "depth", axis=0, tiled=True), at_depth * col_width, col_width, 1
    )
    partial_rows = jnp.dot(columns, query_weight, preferred_element_type=jnp.float32)
    query_sum = lax.psum_scatter(partial_rows, "depth", scatter_dimension=0, tiled=True)
    queries = query_sum.astype(jnp.bfloat16)
    piece = lax.all_gather(queries, "wide", axis=0, tiled=True)
    piece_rows = piece.shape[0]
    indices = jnp.arange(piece_rows, dtype=jnp.int32)
    global_rows = (indices // row_count * halves + at_depth) * row_count + indices % row_count
    owner_rows = jnp.take(cache_slot, global_rows)
    block_count = jnp.take(enc_blocks, global_rows)
    is_owner = owner_rows // (halves * row_count) == at_wide
    same_row = (owner_rows % row_count)[:, None] == jnp.arange(row_count, dtype=jnp.int32)[None, :]
    chosen = (is_owner[:, None] & same_row).astype(jnp.bfloat16)
    answered = attend_pairs(piece, cache_keys, cache_values, chosen, block_count)
    context_sum = lax.psum_scatter(
        answered.astype(jnp.bfloat16), "wide", scatter_dimension=0, tiled=True
    )
    partial_value = jnp.dot(context_sum, output_weight, preferred_element_type=jnp.float32)
    return lax.psum_scatter(partial_value, "narrow", scatter_dimension=1, tiled=True).astype(
        jnp.bfloat16
    )


def solution(mesh):
    placed = (
        P(("wide", "depth"), None),
        P("depth", "narrow"),
        P("narrow", None),
        P(("wide", "depth"), None, "narrow"),
        P(("wide", "depth"), None, "narrow"),
        P(),
        P(),
    )
    return jax.shard_map(
        shards,
        mesh=mesh,
        in_specs=placed,
        out_specs=P(("wide", "depth"), "narrow"),
        check_vma=False,
    )
```

profile of v0, /device:TPU:0, one launch (start us, length us, event | category | flops | bytes accessed | tf_op | source)
XLA Modules:
  0.0 116.5 jit_solution(13722981747352246614)
XLA Ops:
  6.5 0.0 copy-start
  6.5 0.0 reduce-scatter.4.cloned.1.call-start
  6.6 1.3 %dynamic-slice.2 = u32[1]{0:T(128)} dynamic-slice(u32[32]{0:T(128)} %constant.91, u32[]{:T(128)S(6)} %add.52), dynamic_slice_sizes={1} | dynamic-slice | bytes 12
  7.9 1.2 %dynamic-slice = u32[1]{0:T(128)} dynamic-slice(u32[32]{0:T(128)} %constant.87, u32[]{:T(128)S(6)} %add.52), dynamic_slice_sizes={1} | dynamic-slice | bytes 12
  10.5 0.9 fusion.24
  11.3 0.0 copy-done
  11.4 0.6 gather_fusion.1
  12.0 1.3 %gather_fusion = s32[8]{0:T(128)S(1)} fusion(s32[16]{0:T(128)} %param.14, s32[1024]{0:T(1024)S(1)} %pad_clamp_fusion), kind=kCustom, calls=%fused_computation.clone | custom fusion | bytes 96 | tf_op jit(solution)/shard_map/jit(_take)/gather | solution.py:52
  13.4 0.1 iota_compare_fusion
  13.4 0.8 fusion.29
  14.2 5.3 %all-gather = bf16[2,2,4096]{2,1,0:T(2,128)(2,1)S(1)} all-gather(bf16[1,2,4096]{2,1,0:T(2,128)(2,1)S(1)} %fusion.29), channel_id=1, replica_groups=mesh['wide'=4,'narrow'=4,'depth'=2] {'depth'}, dimensions={0}, use_global_device_ids=true | all-gather | bytes 49152 | tf_op jit(solution)/shard_map/all_gather | solution.py:42
  19.6 0.0 copy-start.1
  19.6 3.0 %fusion.27 = f32[4,1024]{1,0:T(4,128)S(1)} fusion(bf16[2048,1024]{1,0:T(8,128)(2,1)} %param.10, bf16[4,4096]{1,0:T(4,128)(2,1)S(1)} %reshape.103, s32[]{:T(128)S(6)} %select_n.37), kind=kOutput, calls=%fused_computation.23 | convolution fusion | flops 16777216 | bytes 4227076 | tf_op jit(solution)/shard_map/dot_general | solution.py:44
  22.6 8.7 %all-reduce = bf16[4,1024]{1,0:T(4,128)(2,1)S(1)} all-reduce(f32[4,1024]{1,0:T(4,128)S(1)} %fusion.27), channel_id=2, replica_groups=mesh['wide'=4,'narrow'=4,'depth'=2] {'depth'}, use_global_device_ids=true, to_apply=%region_1.3.clone | all-reduce | flops 4096 | bytes 24576
  31.3 5.2 %all-gather.1 = bf16[4,2,1024]{2,1,0:T(2,128)(2,1)S(1)} all-gather(bf16[1,2,1024]{2,1,0:T(2,128)(2,1)S(1)} %fusion.30), channel_id=1, replica_groups=mesh['wide'=4,'narrow'=4,'depth'=2] {'wide'}, dimensions={0}, use_global_device_ids=true | all-gather | bytes 20480 | tf_op jit(solution)/shard_map/all_gather | solution.py:47
  36.5 0.1 reshape.81
  36.6 0.0 copy-done.1
  36.6 2.6 %copy.22 = bf16[2,512,1024]{1,2,0:T(8,128)(2,1)} copy(bf16[2,512,1024]{2,1,0:T(8,128)(2,1)S(1)} %copy-done.1) | data formatting | bytes 4194304 | tf_op args[3]
  39.2 2.9 %copy.25 = bf16[2,512,1024]{1,2,0:T(8,128)(2,1)S(1)} copy(bf16[2,512,1024]{2,1,0:T(8,128)(2,1)} %param.13) | data formatting | bytes 4194304 | tf_op args[4]
  42.1 2.2 %fusion.39 = (f32[8,2,16]{0,1,2:T(2,128)S(1)}, f32[8,2,16,512]{3,0,1,2:T(8,128)S(1)}) fusion(bf16[2,512,16,64]{1,3,2,0:T(8,128)(2,1)} %bitcast.28, pred[8,512]{1,0:T(8,128)(4,1)S(1)} %iota_compare_fusion, bf16[8,16,64,1]{2,1,0,3:T(8,128)(2,1)S(1)} %bitcast.30), kind=kOutput, calls=%fused_computation.55 | convolution fusion | flops 17170944 | bytes 2642944 | tf_op jit(solution)/shard_map/sub | solution.py:23
  44.2 0.7 fusion.19
  45.0 0.1 convert_element_type.38
  45.1 11.5 %all-reduce.1 = bf16[8,1024]{1,0:T(8,128)(2,1)S(1)} all-reduce(bf16[8,1024]{1,0:T(8,128)(2,1)S(1)} %convert_element_type.38), channel_id=3, replica_groups=mesh['wide'=4,'narrow'=4,'depth'=2] {'wide'}, use_global_device_ids=true, to_apply=%region_4.6.clone | all-reduce | flops 8192 | bytes 32768
  56.5 8.1 %convolution_bitcast_fusion = f32[4096,2]{1,0:T(8,128)} fusion(bf16[1024,4096]{1,0:T(8,128)(2,1)} %param.11, bf16[8,1024]{1,0:T(8,128)(2,1)S(1)} %all-reduce.1, u32[]{:T(128)S(6)} %multiply.9), kind=kOutput, calls=%fused_computation.3 | convolution fusion | flops 16777216 | bytes 8425476
  64.6 0.0 reduce-scatter.4.cloned.1.call-update
  64.7 43.2 %reduce-scatter.4.cloned.1.call-done = f32[1024,2]{1,0:T(8,128)} async-done(((f32[4096,2]{1,0:T(8,128)}), f32[1024,2]{1,0:T(8,128)}) %reduce-scatter.4.cloned.1.call-update) | async-done | bytes 8208
  107.8 1.8 %copy.33 = bf16[2,1024]{1,0:T(2,128)(2,1)} copy(f32[2,1024]{0,1:T(8,128)} %bitcast.29) | data formatting | bytes 12288
  (10 shorter events, 0.1 us)
Async XLA Ops:
  6.5 4.8 %copy-start = (s32[16]{0:T(128)S(1)}, s32[16]{0:T(128)}, u32[]{:S(2)}) copy-start(s32[16]{0:T(128)} %param.15) | copy-start | bytes 196
  6.5 101.3 %reduce-scatter.4.cloned.1.call-start = ((), (), s32[]{:S(2)}) async-start(), calls=%async_computation.1 | async-start | bytes 2621440
  19.6 17.0 %copy-start.1 = (bf16[2,512,1024]{2,1,0:T(8,128)(2,1)S(1)}, bf16[2,512,1024]{2,1,0:T(8,128)(2,1)}, u32[]{:S(2)}) copy-start(bf16[2,512,1024]{2,1,0:T(8,128)(2,1)} %param.12) | copy-start | bytes 6291460
Sparse Core Ops, SparseCore 0:
  64.8 43.0 reduce-scatter.3
where the time goes:
time: 117 us
  waiting for transfers between devices  43.2 us (37%)
  blocking collectives  30.7 us (26%)
  between operations  14.8 us (13%)
  matrix products  14 us (12%)
  local copies, waits for them, and re-layouts  12 us (10%)
  other arithmetic  1.82 us (2%)
    unnamed x2, waiting for transfers between devices  43.2 us
    unnamed x2, blocking collectives  20.2 us
    unnamed x11, local copies, waits for them, and re-layouts  9.86 us
    unnamed x1, matrix products  8.1 us
    all_gather x1, blocking collectives, shards(): lax.all_gather(normed, 'depth', axis=0, tiled=True)  5.33 us
    all_gather x1, blocking collectives, shards(): piece = lax.all_gather(queries, 'wide', axis=0, tiled=True)  5.21 us
    dot_general x1, matrix products, shards(): jnp.dot(columns, query_weight, preferred_element_type=jnp.float32)  2.99 us
  transfers between devices with their start and end apart: 1, of which 1 were waited for; matrix products, arithmetic and copies ran while one was open for 0% of the time, Pallas kernels for 0%

commit v1 on v0

v1 whole, which is shorter than its diff:
```python
import jax
import jax.numpy as jnp
from jax import lax
from jax.experimental import pallas as pl
from jax.experimental.pallas import tpu as pltpu
from jax.sharding import PartitionSpec as P

HDIM = 64
BLOCK = 128

VMEM = pl.BlockSpec(memory_space=pltpu.VMEM)
SMEM = pl.BlockSpec(memory_space=pltpu.SMEM)


def request_of(slot_ref, slot, lead):
    found = jnp.int32(0)
    for r in lead:
        found = jnp.where(slot_ref[r] == slot, jnp.int32(r), found)
    return found


def norm_kernel(hidden_ref, own_ref, other_ref):
    half = own_ref.shape[1]
    at_depth = lax.axis_index("depth")
    widened = hidden_ref[...].astype(jnp.float32)
    mean_square = jnp.mean(widened * widened, axis=-1, keepdims=True)
    normed = widened * lax.rsqrt(mean_square + 1e-06)
    low, high = normed[:, :half], normed[:, half:]
    first = at_depth == 0
    own_ref[...] = jnp.where(first, low, high).astype(jnp.bfloat16)
    other_ref[...] = jnp.where(first, high, low).astype(jnp.bfloat16)


def query_kernel(sizes, slot_ref, *refs):
    wide, halves, rows = sizes
    pieces = len(refs) - 1 - 4 - 2
    piece_refs, weight_ref = refs[:pieces], refs[pieces]
    out_refs = refs[pieces + 1 : pieces + 5]
    rows_ref, sums_ref = refs[pieces + 5 :]
    at_wide, at_depth = lax.axis_index("wide"), lax.axis_index("depth")
    for k, piece in enumerate(piece_refs):
        rows_ref[k * rows : (k + 1) * rows, :] = piece[...].astype(jnp.float32)
    sums_ref[...] = jnp.dot(
        rows_ref[...].astype(jnp.bfloat16), weight_ref[...], preferred_element_type=jnp.float32
    )
    total = wide * halves * rows
    for k, out in enumerate(out_refs):
        flip_wide, flip_depth = k // 2, k % 2
        peer_wide, peer_depth = at_wide ^ flip_wide, at_depth ^ flip_depth
        for j in range(rows):
            slot = (peer_wide * halves + peer_depth) * rows + j
            r = request_of(slot_ref, slot, range(total))
            from_wide = r // (rows * halves) ^ at_wide
            from_depth = (r // rows) % halves ^ at_depth
            here = (from_wide & 1) == 0
            place = ((from_wide >> 1) * halves + from_depth) * rows + r % rows
            row = sums_ref[pl.ds(place, 1), :]
            out[j : j + 1, :] = jnp.where(here, row, 0.0)


def attend_kernel(sizes, slot_ref, blocks_ref, *refs):
    wide, narrow, halves, rows = sizes
    parts, (keys_ref, values_ref, weight_ref, out_ref) = refs[:4], refs[4:]
    at_wide, at_depth = lax.axis_index("wide"), lax.axis_index("depth")
    cache_len, features = keys_ref.shape[1:]
    heads = features // HDIM
    total = wide * halves * rows
    queries = (parts[0][...] + parts[2][...]) + (parts[1][...] + parts[3][...])
    of_head = (
        lax.broadcasted_iota(jnp.int32, (heads, features), 1) // HDIM
        == lax.broadcasted_iota(jnp.int32, (heads, features), 0)
    )
    positions = lax.broadcasted_iota(jnp.int32, (heads, cache_len), 1)
    contexts = []
    for j in range(rows):
        slot = (at_wide * halves + at_depth) * rows + j
        count = jnp.int32(0)
        for r in range(total):
            count = jnp.where(slot_ref[r] == slot, blocks_ref[r], count)
        spread = jnp.where(of_head, queries[j : j + 1, :], 0.0).astype(jnp.bfloat16)
        scores = lax.dot_general(
            spread, keys_ref[j], (((1,), (1,)), ((), ())), preferred_element_type=jnp.float32
        )
        scores = jnp.where(positions < count * BLOCK, scores, jnp.float32(-1e30))
        row_top = jnp.max(scores, axis=-1, keepdims=True)
        raised = jnp.exp(scores - row_top)
        shares = (raised / jnp.sum(raised, axis=-1, keepdims=True)).astype(jnp.bfloat16)
        mixed = jnp.dot(shares, values_ref[j], preferred_element_type=jnp.float32)
        contexts.append(jnp.sum(jnp.where(of_head, mixed, 0.0), axis=0, keepdims=True))
    padding = jnp.zeros((8 - rows, features), jnp.float32)
    context = jnp.concatenate(contexts + [padding], axis=0).astype(jnp.bfloat16)
    partial = jnp.dot(context, weight_ref[...], preferred_element_type=jnp.float32)
    width = partial.shape[1] // narrow
    for to_wide in range(wide):
        lines = []
        for i in range(rows):
            at = slot_ref[(to_wide * halves + at_depth) * rows + i] - (
                at_wide * halves + at_depth
            ) * rows
            line = jnp.zeros_like(partial[:1])
            for j in range(rows):
                line = jnp.where(at == j, partial[j : j + 1], line)
            lines.append(line)
        block = jnp.concatenate(lines, axis=0).astype(jnp.bfloat16)
        for to_narrow in range(narrow):
            out_ref[to_wide * narrow + to_narrow] = block[
                :, to_narrow * width : (to_narrow + 1) * width
            ]


def sum_kernel(parts_ref, out_ref):
    total = parts_ref[0].astype(jnp.float32)
    for k in range(1, parts_ref.shape[0]):
        total = total + parts_ref[k].astype(jnp.float32)
    out_ref[...] = total.astype(jnp.bfloat16)


def shards(
    hidden_state, query_weight, output_weight, cache_keys, cache_values, enc_blocks, cache_slot
):
    rows = hidden_state.shape[0]
    wide, narrow, halves = (lax.axis_size(name) for name in ("wide", "narrow", "depth"))
    half, features = query_weight.shape
    width = output_weight.shape[1]

    def flipped(x, flip_wide, flip_depth):
        pairs = [
            (w * halves + d, (w ^ flip_wide) * halves + (d ^ flip_depth))
            for w in range(wide)
            for d in range(halves)
        ]
        return lax.ppermute(x, ("wide", "depth"), pairs)

    half_rows = jax.ShapeDtypeStruct((rows, half), jnp.bfloat16)
    own, other = pl.pallas_call(
        norm_kernel,
        out_shape=[half_rows, half_rows],
        in_specs=[VMEM],
        out_specs=[VMEM, VMEM],
    )(hidden_state)
    pieces = []
    for chip in range(wide // 2):
        for flip_depth in range(halves):
            if chip == 0 and flip_depth == 0:
                pieces.append(own)
            else:
                pieces.append(flipped(other if flip_depth else own, chip * 2, flip_depth))
    count = len(pieces) * rows
    sums = jax.ShapeDtypeStruct((rows, features), jnp.float32)
    parts = pl.pallas_call(
        lambda *refs: query_kernel((wide, halves, rows), *refs),
        out_shape=[sums] * 4,
        in_specs=[SMEM] + [VMEM] * (len(pieces) + 1),
        out_specs=[VMEM] * 4,
        scratch_shapes=[
            pltpu.VMEM((count, half), jnp.float32),
            pltpu.VMEM((count, features), jnp.float32),
        ],
    )(cache_slot, *pieces, query_weight)
    arrived = [parts[0]] + [flipped(parts[k], k // 2, k % 2) for k in range(1, 4)]
    spread = pl.pallas_call(
        lambda *refs: attend_kernel((wide, narrow, halves, rows), *refs),
        out_shape=jax.ShapeDtypeStruct((wide * narrow, rows, width // narrow), jnp.bfloat16),
        in_specs=[SMEM, SMEM] + [VMEM] * 7,
        out_specs=VMEM,
    )(cache_slot, enc_blocks, *arrived, cache_keys, cache_values, output_weight)
    gathered = lax.all_to_all(spread, ("wide", "narrow"), 0, 0, tiled=True)
    return pl.pallas_call(
        sum_kernel,
        out_shape=jax.ShapeDtypeStruct((rows, width // narrow), jnp.bfloat16),
        in_specs=[VMEM],
        out_specs=VMEM,
    )(gathered)


def solution(mesh):
    placed = (
        P(("wide", "depth"), None),
        P("depth", "narrow"),
        P("narrow", None),
        P(("wide", "depth"), None, "narrow"),
        P(("wide", "depth"), None, "narrow"),
        P(),
        P(),
    )
    return jax.shard_map(
        shards,
        mesh=mesh,
        in_specs=placed,
        out_specs=P(("wide", "depth"), "narrow"),
        check_vma=False,
    )
```

time: 117 us -> 40.9 us (0.35)
  waiting for transfers between devices: 43.2 us -> 6.43 us
  blocking collectives: 30.7 us -> 11.8 us
  between operations: 14.8 us -> 0.02 us
  Pallas kernels: 0 us -> 14.5 us
  matrix products: 14 us -> 0 us
  local copies, waits for them, and re-layouts: 12 us -> 1.25 us
  starting transfers between devices: 0.01 us -> 6.63 us
  other arithmetic: 1.82 us -> 0 us
    unnamed x2 -> x0, waiting for transfers between devices: 43.2 us -> none
    unnamed x2 -> x0, blocking collectives: 20.2 us -> none
    pallas_call x0 -> x4, Pallas kernels: none -> 14.5 us  [the longest x1 7.96 us: shards(): pl.pallas_call(lambda *refs: attend_kernel((wide, narrow, halves, rows),...]
    all_to_all x0 -> x1, blocking collectives: none -> 11.8 us  [shards(): gathered = lax.all_to_all(spread, ('wide', 'narrow'), 0, 0, tiled=True)]
    all_gather x2 -> x0, blocking collectives: 10.5 us -> none  [the longest x1 5.33 us: shards(): lax.all_gather(normed, 'depth', axis=0, tiled=True)]
    unnamed x11 -> x12, local copies, waits for them, and re-layouts: 9.86 us -> 1.25 us
    unnamed x1 -> x0, matrix products: 8.1 us -> none
    ppermute x0 -> x6, starting transfers between devices: none -> 6.63 us  [flipped(): return lax.ppermute(x, ('wide', 'depth'), pairs)]
  transfers between devices with their start and end apart: 1 -> 6, of which waited for: 1 -> 5; matrix products, arithmetic and copies ran while one was open for 0% -> 0% of each run, Pallas kernels for 0% -> 0%
where the time goes in v1:
time: 40.9 us; the launch traced here: 40.6 us
  Pallas kernels  14.5 us (35%)
  blocking collectives  11.8 us (29%)
  starting transfers between devices  6.63 us (16%)
  waiting for transfers between devices  6.43 us (16%)
  local copies, waits for them, and re-layouts  1.25 us (3%)
    all_to_all x1, blocking collectives, shards(): gathered = lax.all_to_all(spread, ('wide', 'narrow'), 0, 0, tiled=True)  11.8 us
    pallas_call x1, Pallas kernels, shards(): pl.pallas_call(lambda *refs: attend_kernel((wide, narrow, halves, rows),...  7.96 us
    ppermute x6, starting transfers between devices, flipped(): return lax.ppermute(x, ('wide', 'depth'), pairs)  6.63 us
    ppermute x6, waiting for transfers between devices, flipped(): return lax.ppermute(x, ('wide', 'depth'), pairs)  6.43 us
    pallas_call x1, Pallas kernels, shards(): pl.pallas_call(lambda *refs: query_kernel((wide, halves, rows), *refs), o...  3.61 us
    pallas_call x1, Pallas kernels, shards(): pl.pallas_call(sum_kernel, out_shape=jax.ShapeDtypeStruct((rows, width //...  1.46 us
    pallas_call x1, Pallas kernels, shards(): pl.pallas_call(norm_kernel, out_shape=[half_rows, half_rows], in_specs=[V...  1.45 us
    unnamed x12, local copies, waits for them, and re-layouts  1.25 us
  transfers between devices with their start and end apart: 6, of which 5 were waited for; matrix products, arithmetic and copies ran while one was open for 0% of the time, Pallas kernels for 0%

profile of v1, /device:TPU:0, one launch (start us, length us, event | category | flops | bytes accessed | tf_op | source)
XLA Modules:
  0.0 40.6 jit_solution(10533484799281540747)
XLA Ops:
  0.0 1.5 %shard_map.73 = (bf16[2,2048]{1,0:T(2,128)(2,1)}, bf16[2,2048]{1,0:T(2,128)(2,1)}) custom-call(bf16[2,4096]{1,0:T(2,128)(2,1)} %hidden_ref.1), custom_call_target="tpu_custom_call" | custom-call | tf_op jit(solution)/shard_map/pallas_call | solution.py:135
  1.5 3.0 %collective-permute-start.1 = (bf16[2,2048]{1,0:T(2,128)(2,1)}, bf16[2,2048]{1,0:T(2,128)(2,1)S(1)}, u32[]{:S(2)}, u32[]{:S(2)}) collective-permute-start(bf16[2,2048]{1,0:T(2,128)(2,1)} %get-tuple-element.11.refs_1_), channel_id=1, source_target_pairs={{0,16},{1,17},{8,24},{9,25},{16,0},{17,1},{24,8},{25,9},{2,18},{3,... | collective-permute-start | bytes 24584 | tf_op jit(solution)/shard_map/ppermute | solution.py:132
  4.5 1.4 %collective-permute-start.2 = (bf16[2,2048]{1,0:T(2,128)(2,1)}, bf16[2,2048]{1,0:T(2,128)(2,1)S(1)}, u32[]{:S(2)}, u32[]{:S(2)}) collective-permute-start(bf16[2,2048]{1,0:T(2,128)(2,1)} %get-tuple-element.12), channel_id=1, source_target_pairs={{0,17},{1,16},{8,25},{9,24},{16,1},{17,0},{24,9},{25,8},{2,19},{3,... | collective-permute-start | bytes 24584 | tf_op jit(solution)/shard_map/ppermute | solution.py:132
  5.9 0.1 collective-permute-start
  5.9 0.3 collective-permute-done.1.refs_3_
  6.3 0.0 copy-start
  6.3 2.9 %collective-permute-done.2.refs_4_ = bf16[2,2048]{1,0:T(2,128)(2,1)S(1)} collective-permute-done((bf16[2,2048]{1,0:T(2,128)(2,1)}, bf16[2,2048]{1,0:T(2,128)(2,1)S(1)}, u32[]{:S(2)}, u32[]{:S(2)}) %collective-permute-start.2) | collective-permute-done | bytes 8224 | tf_op jit(solution)/shard_map/ppermute | solution.py:132
  9.2 0.0 copy-start.2
  9.2 0.5 %collective-permute-done.refs_2_ = bf16[2,2048]{1,0:T(2,128)(2,1)S(1)} collective-permute-done((bf16[2,2048]{1,0:T(2,128)(2,1)}, bf16[2,2048]{1,0:T(2,128)(2,1)S(1)}, u32[]{:S(2)}, u32[]{:S(2)}) %collective-permute-start) | collective-permute-done | bytes 8224 | tf_op jit(solution)/shard_map/ppermute | solution.py:132
  9.7 0.0 copy-done
  9.8 0.1 copy-done.2
  9.8 0.0 copy-start.4
  9.8 0.6 %copy-done.4 = bf16[2,2048]{1,0:T(2,128)(2,1)} copy-done((bf16[2,2048]{1,0:T(2,128)(2,1)}, bf16[2,2048]{1,0:T(2,128)(2,1)S(1)}, u32[]{:S(2)}) %copy-start.4) | copy-done | bytes 8216
  10.4 3.6 %shard_map.74 = (f32[2,1024]{1,0:T(2,128)}, f32[2,1024]{1,0:T(2,128)}, f32[2,1024]{1,0:T(2,128)}, f32[2,1024]{1,0:T(2,128)}) custom-call(s32[16]{0:T(128)} %refs_0_.3, bf16[2,2048]{1,0:T(2,128)(2,1)} %get-tuple-element.11.refs_1_, bf16[2,2048]{1,0:T(2,128)(2,1)} %copy-done.4, bf16[2,2048]{1,0:T(2,128)(2,1)} %copy-done, bf16[2,2048]{1,0:T(2,128)(2,1)} %copy-done.2, ...), custom_call_target="tpu_custom_call" | custom-call | tf_op jit(solution)/shard_map/pallas_call | solution.py:150
  14.0 1.5 %collective-permute-start.3 = (f32[2,1024]{1,0:T(2,128)}, f32[2,1024]{1,0:T(2,128)S(1)}, u32[]{:S(2)}, u32[]{:S(2)}) collective-permute-start(f32[2,1024]{1,0:T(2,128)} %get-tuple-element.14), channel_id=1, source_target_pairs={{0,1},{1,0},{8,9},{9,8},{16,17},{17,16},{24,25},{25,24},{2,3},{3,2... | collective-permute-start | bytes 24584 | tf_op jit(solution)/shard_map/ppermute | solution.py:132
  15.5 0.0 collective-permute-start.4
  15.5 0.6 %collective-permute-start.5 = (f32[2,1024]{1,0:T(2,128)}, f32[2,1024]{1,0:T(2,128)S(1)}, u32[]{:S(2)}, u32[]{:S(2)}) collective-permute-start(f32[2,1024]{1,0:T(2,128)} %get-tuple-element.16), channel_id=1, source_target_pairs={{0,9},{1,8},{8,1},{9,0},{16,25},{17,24},{24,17},{25,16},{2,11},{3,... | collective-permute-start | bytes 24584 | tf_op jit(solution)/shard_map/ppermute | solution.py:132
  16.1 1.7 %collective-permute-done.3.refs_3_ = f32[2,1024]{1,0:T(2,128)S(1)} collective-permute-done((f32[2,1024]{1,0:T(2,128)}, f32[2,1024]{1,0:T(2,128)S(1)}, u32[]{:S(2)}, u32[]{:S(2)}) %collective-permute-start.3) | collective-permute-done | bytes 8224 | tf_op jit(solution)/shard_map/ppermute | solution.py:132
  17.9 0.0 copy-start.1
  17.9 0.0 collective-permute-done.4.refs_4_
  17.9 0.0 copy-start.3
  17.9 0.9 %collective-permute-done.5.refs_5_ = f32[2,1024]{1,0:T(2,128)S(1)} collective-permute-done((f32[2,1024]{1,0:T(2,128)}, f32[2,1024]{1,0:T(2,128)S(1)}, u32[]{:S(2)}, u32[]{:S(2)}) %collective-permute-start.5) | collective-permute-done | bytes 8224 | tf_op jit(solution)/shard_map/ppermute | solution.py:132
  18.8 0.0 copy-start.5
  18.8 0.0 copy-done.1
  18.8 0.0 copy-done.3
  18.8 0.6 %copy-done.5 = f32[2,1024]{1,0:T(2,128)} copy-done((f32[2,1024]{1,0:T(2,128)}, f32[2,1024]{1,0:T(2,128)S(1)}, u32[]{:S(2)}) %copy-start.5) | copy-done | bytes 8216
  19.4 8.0 %shard_map.75 = bf16[16,2,1024]{2,1,0:T(2,128)(2,1)} custom-call(s32[16]{0:T(128)} %refs_0_.3, s32[16]{0:T(128)} %refs_1_.1, f32[2,1024]{1,0:T(2,128)} %get-tuple-element.13.refs_2_, f32[2,1024]{1,0:T(2,128)} %copy-done.1, f32[2,1024]{1,0:T(2,128)} %copy-done.3, f32[2,1024]{1,0:T(2,128)} %copy-done.5, bf16[2,512,1024]{2,1,0:T(8,128)(2,1)} %refs_6_.1, ...), custom_call_target="tpu_custom_call" | custom-call | tf_op jit(solution)/shard_map/pallas_call | solution.py:161
  27.3 11.8 %all_to_all.5.parts_ref = bf16[16,2,1024]{2,1,0:T(2,128)(2,1)} all-to-all(bf16[16,2,1024]{2,1,0:T(2,128)(2,1)} %shard_map.75), channel_id=1, replica_groups=mesh['wide'=4,'narrow'=4,'depth'=2] {'wide','narrow'}, dimensions={0} | all-to-all | bytes 131072 | tf_op jit(solution)/shard_map/all_to_all | solution.py:167
  39.2 1.5 %shard_map.76 = bf16[2,1024]{1,0:T(2,128)(2,1)} custom-call(bf16[16,2,1024]{2,1,0:T(2,128)(2,1)} %all_to_all.5.parts_ref), custom_call_target="tpu_custom_call" | custom-call | tf_op jit(solution)/shard_map/pallas_call | solution.py:168
Async XLA Ops:
  1.5 4.8 %collective-permute-start.1 = (bf16[2,2048]{1,0:T(2,128)(2,1)}, bf16[2,2048]{1,0:T(2,128)(2,1)S(1)}, u32[]{:S(2)}, u32[]{:S(2)}) collective-permute-start(bf16[2,2048]{1,0:T(2,128)(2,1)} %get-tuple-element.11.refs_1_), channel_id=1, source_target_pairs={{0,16},{1,17},{8,24},{9,25},{16,0},{17,1},{24,8},{25,9},{2,18},{3,... | collective-permute-start | bytes 24584 | tf_op jit(solution)/shard_map/ppermute | solution.py:132
  4.5 4.8 %collective-permute-start.2 = (bf16[2,2048]{1,0:T(2,128)(2,1)}, bf16[2,2048]{1,0:T(2,128)(2,1)S(1)}, u32[]{:S(2)}, u32[]{:S(2)}) collective-permute-start(bf16[2,2048]{1,0:T(2,128)(2,1)} %get-tuple-element.12), channel_id=1, source_target_pairs={{0,17},{1,16},{8,25},{9,24},{16,1},{17,0},{24,9},{25,8},{2,19},{3,... | collective-permute-start | bytes 24584 | tf_op jit(solution)/shard_map/ppermute | solution.py:132
  5.9 3.9 %collective-permute-start = (bf16[2,2048]{1,0:T(2,128)(2,1)}, bf16[2,2048]{1,0:T(2,128)(2,1)S(1)}, u32[]{:S(2)}, u32[]{:S(2)}) collective-permute-start(bf16[2,2048]{1,0:T(2,128)(2,1)} %get-tuple-element.12), channel_id=1, source_target_pairs={{0,1},{1,0},{8,9},{9,8},{16,17},{17,16},{24,25},{25,24},{2,3},{3,2... | collective-permute-start | bytes 24584 | tf_op jit(solution)/shard_map/ppermute | solution.py:132
  6.3 3.5 %copy-start = (bf16[2,2048]{1,0:T(2,128)(2,1)}, bf16[2,2048]{1,0:T(2,128)(2,1)S(1)}, u32[]{:S(2)}) copy-start(bf16[2,2048]{1,0:T(2,128)(2,1)S(1)} %collective-permute-done.1.refs_3_) | copy-start | bytes 24580
  9.2 0.6 %copy-start.2 = (bf16[2,2048]{1,0:T(2,128)(2,1)}, bf16[2,2048]{1,0:T(2,128)(2,1)S(1)}, u32[]{:S(2)}) copy-start(bf16[2,2048]{1,0:T(2,128)(2,1)S(1)} %collective-permute-done.2.refs_4_) | copy-start | bytes 24580
  9.8 0.6 %copy-start.4 = (bf16[2,2048]{1,0:T(2,128)(2,1)}, bf16[2,2048]{1,0:T(2,128)(2,1)S(1)}, u32[]{:S(2)}) copy-start(bf16[2,2048]{1,0:T(2,128)(2,1)S(1)} %collective-permute-done.refs_2_) | copy-start | bytes 24580
  14.0 3.9 %collective-permute-start.3 = (f32[2,1024]{1,0:T(2,128)}, f32[2,1024]{1,0:T(2,128)S(1)}, u32[]{:S(2)}, u32[]{:S(2)}) collective-permute-start(f32[2,1024]{1,0:T(2,128)} %get-tuple-element.14), channel_id=1, source_target_pairs={{0,1},{1,0},{8,9},{9,8},{16,17},{17,16},{24,25},{25,24},{2,3},{3,2... | collective-permute-start | bytes 24584 | tf_op jit(solution)/shard_map/ppermute | solution.py:132
  15.5 2.4 %collective-permute-start.4 = (f32[2,1024]{1,0:T(2,128)}, f32[2,1024]{1,0:T(2,128)S(1)}, u32[]{:S(2)}, u32[]{:S(2)}) collective-permute-start(f32[2,1024]{1,0:T(2,128)} %get-tuple-element.15), channel_id=1, source_target_pairs={{0,8},{1,9},{8,0},{9,1},{16,24},{17,25},{24,16},{25,17},{2,10},{3,... | collective-permute-start | bytes 24584 | tf_op jit(solution)/shard_map/ppermute | solution.py:132
  15.5 3.3 %collective-permute-start.5 = (f32[2,1024]{1,0:T(2,128)}, f32[2,1024]{1,0:T(2,128)S(1)}, u32[]{:S(2)}, u32[]{:S(2)}) collective-permute-start(f32[2,1024]{1,0:T(2,128)} %get-tuple-element.16), channel_id=1, source_target_pairs={{0,9},{1,8},{8,1},{9,0},{16,25},{17,24},{24,17},{25,16},{2,11},{3,... | collective-permute-start | bytes 24584 | tf_op jit(solution)/shard_map/ppermute | solution.py:132
  17.9 0.9 %copy-start.1 = (f32[2,1024]{1,0:T(2,128)}, f32[2,1024]{1,0:T(2,128)S(1)}, u32[]{:S(2)}) copy-start(f32[2,1024]{1,0:T(2,128)S(1)} %collective-permute-done.3.refs_3_) | copy-start | bytes 24580
  17.9 0.9 %copy-start.3 = (f32[2,1024]{1,0:T(2,128)}, f32[2,1024]{1,0:T(2,128)S(1)}, u32[]{:S(2)}) copy-start(f32[2,1024]{1,0:T(2,128)S(1)} %collective-permute-done.4.refs_4_) | copy-start | bytes 24580
  18.8 0.6 %copy-start.5 = (f32[2,1024]{1,0:T(2,128)}, f32[2,1024]{1,0:T(2,128)S(1)}, u32[]{:S(2)}) copy-start(f32[2,1024]{1,0:T(2,128)S(1)} %collective-permute-done.5.refs_5_) | copy-start | bytes 24580

commit v2 on v1

--- a/solution.py
+++ b/solution.py
@@ -8,6 +8,7 @@
 HDIM = 64
 BLOCK = 128
 
+MIB = 1 << 20
 VMEM = pl.BlockSpec(memory_space=pltpu.VMEM)
 SMEM = pl.BlockSpec(memory_space=pltpu.SMEM)
 
@@ -137,6 +138,7 @@
         out_shape=[half_rows, half_rows],
         in_specs=[VMEM],
         out_specs=[VMEM, VMEM],
+        compiler_params=pltpu.CompilerParams(vmem_limit_bytes=MIB),
     )(hidden_state)
     pieces = []
     for chip in range(wide // 2):
@@ -156,6 +158,7 @@
             pltpu.VMEM((count, half), jnp.float32),
             pltpu.VMEM((count, features), jnp.float32),
         ],
+        compiler_params=pltpu.CompilerParams(vmem_limit_bytes=6 * MIB),
     )(cache_slot, *pieces, query_weight)
     arrived = [parts[0]] + [flipped(parts[k], k // 2, k % 2) for k in range(1, 4)]
     spread = pl.pallas_call(
@@ -163,6 +166,7 @@
         out_shape=jax.ShapeDtypeStruct((wide * narrow, rows, width // narrow), jnp.bfloat16),
         in_specs=[SMEM, SMEM] + [VMEM] * 7,
         out_specs=VMEM,
+        compiler_params=pltpu.CompilerParams(vmem_limit_bytes=16 * MIB),
     )(cache_slot, enc_blocks, *arrived, cache_keys, cache_values, output_weight)
     gathered = lax.all_to_all(spread, ("wide", "narrow"), 0, 0, tiled=True)
     return pl.pallas_call(
@@ -170,6 +174,7 @@
         out_shape=jax.ShapeDtypeStruct((rows, width // narrow), jnp.bfloat16),
         in_specs=[VMEM],
         out_specs=VMEM,
+        compiler_params=pltpu.CompilerParams(vmem_limit_bytes=MIB),
     )(gathered)
 
 

time: 40.9 us -> 36.8 us (0.90)
  Pallas kernels: 14.5 us -> 5.21 us
  local copies, waits for them, and re-layouts: 1.25 us -> 6.95 us
  waiting for transfers between devices: 6.43 us -> 5.44 us
    unnamed x12 -> x16, local copies, waits for them, and re-layouts: 1.25 us -> 6.95 us
    pallas_call x1, Pallas kernels: 7.96 us -> 3.17 us  [shards(): pl.pallas_call(lambda *refs: attend_kernel((wide, narrow, halves, rows),...]
    pallas_call x1, Pallas kernels: 3.61 us -> 1.28 us  [shards(): pl.pallas_call(lambda *refs: query_kernel((wide, halves, rows), *refs), o...]
    pallas_call x1, Pallas kernels: 1.45 us -> 0.14 us  [shards(): pl.pallas_call(norm_kernel, out_shape=[half_rows, half_rows], in_specs=[V...]
    ppermute x6, waiting for transfers between devices: 6.43 us -> 5.44 us  [flipped(): return lax.ppermute(x, ('wide', 'depth'), pairs)]
    pallas_call x1, Pallas kernels: 1.46 us -> 0.62 us  [shards(): pl.pallas_call(sum_kernel, out_shape=jax.ShapeDtypeStruct((rows, width //...]
where the time goes in v2:
time: 36.8 us; the launch traced here: 36.5 us
  blocking collectives  12.1 us (33%)
  local copies, waits for them, and re-layouts  6.95 us (19%)
  starting transfers between devices  6.81 us (19%)
  waiting for transfers between devices  5.44 us (15%)
  Pallas kernels  5.21 us (14%)
    all_to_all x1, blocking collectives, shards(): gathered = lax.all_to_all(spread, ('wide', 'narrow'), 0, 0, tiled=True)  12.1 us
    unnamed x16, local copies, waits for them, and re-layouts  6.95 us
    ppermute x6, starting transfers between devices, flipped(): return lax.ppermute(x, ('wide', 'depth'), pairs)  6.81 us
    ppermute x6, waiting for transfers between devices, flipped(): return lax.ppermute(x, ('wide', 'depth'), pairs)  5.44 us
    pallas_call x1, Pallas kernels, shards(): pl.pallas_call(lambda *refs: attend_kernel((wide, narrow, halves, rows),...  3.17 us
    pallas_call x1, Pallas kernels, shards(): pl.pallas_call(lambda *refs: query_kernel((wide, halves, rows), *refs), o...  1.28 us
  transfers between devices with their start and end apart: 6, of which 5 were waited for; matrix products, arithmetic and copies ran while one was open for 0% of the time, Pallas kernels for 0%

profile of v2, /device:TPU:0, one launch (start us, length us, event | category | flops | bytes accessed | tf_op | source)
XLA Modules:
  0.0 36.5 jit_solution(10076769450485407680)
XLA Ops:
  0.0 0.0 copy-start.4
  0.0 0.7 %copy-done.4 = bf16[2,4096]{1,0:T(2,128)(2,1)S(1)} copy-done((bf16[2,4096]{1,0:T(2,128)(2,1)S(1)}, bf16[2,4096]{1,0:T(2,128)(2,1)}, u32[]{:S(2)}) %copy-start.4) | copy-done | bytes 16408
  0.7 0.0 copy-start.6
  0.7 0.0 copy-start.7
  0.7 0.1 shard_map.73
  0.9 3.1 %collective-permute-start.1 = (bf16[2,2048]{1,0:T(2,128)(2,1)S(1)}, bf16[2,2048]{1,0:T(2,128)(2,1)S(1)}, u32[]{:S(2)}, u32[]{:S(2)}) collective-permute-start(bf16[2,2048]{1,0:T(2,128)(2,1)S(1)} %get-tuple-element.11.refs_1_), channel_id=1, source_target_pairs={{0,16},{1,17},{8,24},{9,25},{16,0},{17,1},{24,8},{25,9},{2,18},{3,... | collective-permute-start | bytes 24584 | tf_op jit(solution)/shard_map/ppermute | solution.py:133
  3.9 1.4 %collective-permute-start.2 = (bf16[2,2048]{1,0:T(2,128)(2,1)S(1)}, bf16[2,2048]{1,0:T(2,128)(2,1)S(1)}, u32[]{:S(2)}, u32[]{:S(2)}) collective-permute-start(bf16[2,2048]{1,0:T(2,128)(2,1)S(1)} %get-tuple-element.12), channel_id=1, source_target_pairs={{0,17},{1,16},{8,25},{9,24},{16,1},{17,0},{24,9},{25,8},{2,19},{3,... | collective-permute-start | bytes 24584 | tf_op jit(solution)/shard_map/ppermute | solution.py:133
  5.4 0.1 collective-permute-start
  5.5 0.1 collective-permute-done.1.refs_3_
  5.6 2.9 %collective-permute-done.2.refs_4_ = bf16[2,2048]{1,0:T(2,128)(2,1)S(1)} collective-permute-done((bf16[2,2048]{1,0:T(2,128)(2,1)S(1)}, bf16[2,2048]{1,0:T(2,128)(2,1)S(1)}, u32[]{:S(2)}, u32[]{:S(2)}) %collective-permute-start.2) | collective-permute-done | bytes 8224 | tf_op jit(solution)/shard_map/ppermute | solution.py:133
  8.5 0.5 %collective-permute-done.refs_2_ = bf16[2,2048]{1,0:T(2,128)(2,1)S(1)} collective-permute-done((bf16[2,2048]{1,0:T(2,128)(2,1)S(1)}, bf16[2,2048]{1,0:T(2,128)(2,1)S(1)}, u32[]{:S(2)}, u32[]{:S(2)}) %collective-permute-start) | collective-permute-done | bytes 8224 | tf_op jit(solution)/shard_map/ppermute | solution.py:133
  9.0 0.0 copy-start.1
  9.0 2.2 %copy-done.1 = bf16[2048,1024]{1,0:T(8,128)(2,1)S(1)} copy-done((bf16[2048,1024]{1,0:T(8,128)(2,1)S(1)}, bf16[2048,1024]{1,0:T(8,128)(2,1)}, u32[]{:S(2)}) %copy-start.1) | copy-done | bytes 4194328
  11.2 0.0 copy-start.5
  11.2 0.7 %copy-done.5 = s32[16]{0:T(128)S(1)} copy-done((s32[16]{0:T(128)S(1)}, s32[16]{0:T(128)}, u32[]{:S(2)}) %copy-start.5) | copy-done | bytes 88
  11.9 0.0 copy-start.2
  11.9 1.3 %shard_map.74 = (f32[2,1024]{1,0:T(2,128)S(1)}, f32[2,1024]{1,0:T(2,128)S(1)}, f32[2,1024]{1,0:T(2,128)S(1)}, f32[2,1024]{1,0:T(2,128)S(1)}) custom-call(s32[16]{0:T(128)S(1)} %copy-done.5, bf16[2,2048]{1,0:T(2,128)(2,1)S(1)} %get-tuple-element.11.refs_1_, bf16[2,2048]{1,0:T(2,128)(2,1)S(1)} %collective-permute-done.refs_2_, ...), custom_call_target="tpu_custom_call" | custom-call | tf_op jit(solution)/shard_map/pallas_call | solution.py:152
  13.2 1.0 %collective-permute-start.3 = (f32[2,1024]{1,0:T(2,128)S(1)}, f32[2,1024]{1,0:T(2,128)S(1)}, u32[]{:S(2)}, u32[]{:S(2)}) collective-permute-start(f32[2,1024]{1,0:T(2,128)S(1)} %get-tuple-element.14), channel_id=1, source_target_pairs={{0,1},{1,0},{8,9},{9,8},{16,17},{17,16},{24,25},{25,24},{2,3},{3,2... | collective-permute-start | bytes 24584 | tf_op jit(solution)/shard_map/ppermute | solution.py:133
  14.2 0.0 collective-permute-start.4
  14.2 1.2 %collective-permute-start.5 = (f32[2,1024]{1,0:T(2,128)S(1)}, f32[2,1024]{1,0:T(2,128)S(1)}, u32[]{:S(2)}, u32[]{:S(2)}) collective-permute-start(f32[2,1024]{1,0:T(2,128)S(1)} %get-tuple-element.16), channel_id=1, source_target_pairs={{0,9},{1,8},{8,1},{9,0},{16,25},{17,24},{24,17},{25,16},{2,11},{3,... | collective-permute-start | bytes 24584 | tf_op jit(solution)/shard_map/ppermute | solution.py:133
  15.4 1.5 %collective-permute-done.3.refs_3_ = f32[2,1024]{1,0:T(2,128)S(1)} collective-permute-done((f32[2,1024]{1,0:T(2,128)S(1)}, f32[2,1024]{1,0:T(2,128)S(1)}, u32[]{:S(2)}, u32[]{:S(2)}) %collective-permute-start.3) | collective-permute-done | bytes 8224 | tf_op jit(solution)/shard_map/ppermute | solution.py:133
  16.9 0.0 collective-permute-done.4.refs_4_
  16.9 0.4 %collective-permute-done.5.refs_5_ = f32[2,1024]{1,0:T(2,128)S(1)} collective-permute-done((f32[2,1024]{1,0:T(2,128)S(1)}, f32[2,1024]{1,0:T(2,128)S(1)}, u32[]{:S(2)}, u32[]{:S(2)}) %collective-permute-start.5) | collective-permute-done | bytes 8224 | tf_op jit(solution)/shard_map/ppermute | solution.py:133
  17.3 0.0 copy-done.6
  17.3 0.0 copy-done.7
  17.3 0.0 copy-done.2
  17.3 0.0 copy-done.3
  17.3 0.0 copy-start
  17.3 3.4 %copy-done = bf16[1024,4096]{1,0:T(8,128)(2,1)S(1)} copy-done((bf16[1024,4096]{1,0:T(8,128)(2,1)S(1)}, bf16[1024,4096]{1,0:T(8,128)(2,1)}, u32[]{:S(2)}) %copy-start) | copy-done | bytes 8388632
  20.7 3.2 %shard_map.75 = bf16[16,2,1024]{2,1,0:T(2,128)(2,1)S(1)} custom-call(s32[16]{0:T(128)S(1)} %copy-done.6, s32[16]{0:T(128)S(1)} %copy-done.7, f32[2,1024]{1,0:T(2,128)S(1)} %get-tuple-element.13.refs_2_, f32[2,1024]{1,0:T(2,128)S(1)} %collective-permute-done.3.refs_3_, f32[2,1024]{1,0:T(2,128)S(1)} %collective-permute-done.4.refs_4_, ...), custom_call_target="tpu_custom_call" | custom-call | tf_op jit(solution)/shard_map/pallas_call | solution.py:164
  23.8 12.1 %all_to_all.5.parts_ref = bf16[16,2,1024]{2,1,0:T(2,128)(2,1)S(1)} all-to-all(bf16[16,2,1024]{2,1,0:T(2,128)(2,1)S(1)} %shard_map.75), channel_id=1, replica_groups=mesh['wide'=4,'narrow'=4,'depth'=2] {'wide','narrow'}, dimensions={0} | all-to-all | bytes 131072 | tf_op jit(solution)/shard_map/all_to_all | solution.py:171
  35.9 0.6 %shard_map.76 = bf16[2,1024]{1,0:T(2,128)(2,1)} custom-call(bf16[16,2,1024]{2,1,0:T(2,128)(2,1)S(1)} %all_to_all.5.parts_ref), custom_call_target="tpu_custom_call" | custom-call | tf_op jit(solution)/shard_map/pallas_call | solution.py:172
  (1 shorter events, 0.0 us)
Async XLA Ops:
  0.0 0.7 %copy-start.4 = (bf16[2,4096]{1,0:T(2,128)(2,1)S(1)}, bf16[2,4096]{1,0:T(2,128)(2,1)}, u32[]{:S(2)}) copy-start(bf16[2,4096]{1,0:T(2,128)(2,1)} %hidden_ref.1) | copy-start | bytes 49156
  0.7 16.5 %copy-start.6 = (s32[16]{0:T(128)S(1)}, s32[16]{0:T(128)}, u32[]{:S(2)}) copy-start(s32[16]{0:T(128)} %refs_0_.3) | copy-start | bytes 196
  0.7 16.5 %copy-start.7 = (s32[16]{0:T(128)S(1)}, s32[16]{0:T(128)}, u32[]{:S(2)}) copy-start(s32[16]{0:T(128)} %refs_1_.1) | copy-start | bytes 196
  0.9 4.7 %collective-permute-start.1 = (bf16[2,2048]{1,0:T(2,128)(2,1)S(1)}, bf16[2,2048]{1,0:T(2,128)(2,1)S(1)}, u32[]{:S(2)}, u32[]{:S(2)}) collective-permute-start(bf16[2,2048]{1,0:T(2,128)(2,1)S(1)} %get-tuple-element.11.refs_1_), channel_id=1, source_target_pairs={{0,16},{1,17},{8,24},{9,25},{16,0},{17,1},{24,8},{25,9},{2,18},{3,... | collective-permute-start | bytes 24584 | tf_op jit(solution)/shard_map/ppermute | solution.py:133
  3.9 4.5 %collective-permute-start.2 = (bf16[2,2048]{1,0:T(2,128)(2,1)S(1)}, bf16[2,2048]{1,0:T(2,128)(2,1)S(1)}, u32[]{:S(2)}, u32[]{:S(2)}) collective-permute-start(bf16[2,2048]{1,0:T(2,128)(2,1)S(1)} %get-tuple-element.12), channel_id=1, source_target_pairs={{0,17},{1,16},{8,25},{9,24},{16,1},{17,0},{24,9},{25,8},{2,19},{3,... | collective-permute-start | bytes 24584 | tf_op jit(solution)/shard_map/ppermute | solution.py:133
  5.4 3.7 %collective-permute-start = (bf16[2,2048]{1,0:T(2,128)(2,1)S(1)}, bf16[2,2048]{1,0:T(2,128)(2,1)S(1)}, u32[]{:S(2)}, u32[]{:S(2)}) collective-permute-start(bf16[2,2048]{1,0:T(2,128)(2,1)S(1)} %get-tuple-element.12), channel_id=1, source_target_pairs={{0,1},{1,0},{8,9},{9,8},{16,17},{17,16},{24,25},{25,24},{2,3},{3,2... | collective-permute-start | bytes 24584 | tf_op jit(solution)/shard_map/ppermute | solution.py:133
  9.0 2.2 %copy-start.1 = (bf16[2048,1024]{1,0:T(8,128)(2,1)S(1)}, bf16[2048,1024]{1,0:T(8,128)(2,1)}, u32[]{:S(2)}) copy-start(bf16[2048,1024]{1,0:T(8,128)(2,1)} %refs_5_.1) | copy-start | bytes 12582916
  11.2 0.7 %copy-start.5 = (s32[16]{0:T(128)S(1)}, s32[16]{0:T(128)}, u32[]{:S(2)}) copy-start(s32[16]{0:T(128)} %refs_0_.3) | copy-start | bytes 196
  11.9 5.4 %copy-start.2 = (bf16[2,512,1024]{2,1,0:T(8,128)(2,1)S(1)}, bf16[2,512,1024]{2,1,0:T(8,128)(2,1)}, u32[]{:S(2)}) copy-start(bf16[2,512,1024]{2,1,0:T(8,128)(2,1)} %refs_6_.1) | copy-start | bytes 6291460
  11.9 5.4 %copy-start.3 = (bf16[2,512,1024]{2,1,0:T(8,128)(2,1)S(1)}, bf16[2,512,1024]{2,1,0:T(8,128)(2,1)}, u32[]{:S(2)}) copy-start(bf16[2,512,1024]{2,1,0:T(8,128)(2,1)} %refs_7_.1) | copy-start | bytes 6291460
  13.2 3.7 %collective-permute-start.3 = (f32[2,1024]{1,0:T(2,128)S(1)}, f32[2,1024]{1,0:T(2,128)S(1)}, u32[]{:S(2)}, u32[]{:S(2)}) collective-permute-start(f32[2,1024]{1,0:T(2,128)S(1)} %get-tuple-element.14), channel_id=1, source_target_pairs={{0,1},{1,0},{8,9},{9,8},{16,17},{17,16},{24,25},{25,24},{2,3},{3,2... | collective-permute-start | bytes 24584 | tf_op jit(solution)/shard_map/ppermute | solution.py:133
  14.2 2.7 %collective-permute-start.4 = (f32[2,1024]{1,0:T(2,128)S(1)}, f32[2,1024]{1,0:T(2,128)S(1)}, u32[]{:S(2)}, u32[]{:S(2)}) collective-permute-start(f32[2,1024]{1,0:T(2,128)S(1)} %get-tuple-element.15), channel_id=1, source_target_pairs={{0,8},{1,9},{8,0},{9,1},{16,24},{17,25},{24,16},{25,17},{2,10},{3,... | collective-permute-start | bytes 24584 | tf_op jit(solution)/shard_map/ppermute | solution.py:133
  14.2 3.1 %collective-permute-start.5 = (f32[2,1024]{1,0:T(2,128)S(1)}, f32[2,1024]{1,0:T(2,128)S(1)}, u32[]{:S(2)}, u32[]{:S(2)}) collective-permute-start(f32[2,1024]{1,0:T(2,128)S(1)} %get-tuple-element.16), channel_id=1, source_target_pairs={{0,9},{1,8},{8,1},{9,0},{16,25},{17,24},{24,17},{25,16},{2,11},{3,... | collective-permute-start | bytes 24584 | tf_op jit(solution)/shard_map/ppermute | solution.py:133
  17.3 3.4 %copy-start = (bf16[1024,4096]{1,0:T(8,128)(2,1)S(1)}, bf16[1024,4096]{1,0:T(8,128)(2,1)}, u32[]{:S(2)}) copy-start(bf16[1024,4096]{1,0:T(8,128)(2,1)} %refs_8_.1) | copy-start | bytes 25165828

commit v3 on v2

--- a/solution.py
+++ b/solution.py
@@ -139,6 +139,7 @@
         in_specs=[VMEM],
         out_specs=[VMEM, VMEM],
         compiler_params=pltpu.CompilerParams(vmem_limit_bytes=MIB),
+        cost_estimate=pl.CostEstimate(flops=10**10, bytes_accessed=0, transcendentals=0),
     )(hidden_state)
     pieces = []
     for chip in range(wide // 2):

time: 36.8 us -> 30.7 us (0.83)
  local copies, waits for them, and re-layouts: 6.95 us -> 0.9 us
    unnamed x16 -> x14, local copies, waits for them, and re-layouts: 6.95 us -> 0.9 us
where the time goes in v3:
time: 30.7 us; the launch traced here: 30.5 us
  blocking collectives  12.1 us (39%)
  starting transfers between devices  6.81 us (22%)
  waiting for transfers between devices  5.44 us (18%)
  Pallas kernels  5.21 us (17%)
  local copies, waits for them, and re-layouts  0.9 us (3%)
    all_to_all x1, blocking collectives, shards(): gathered = lax.all_to_all(spread, ('wide', 'narrow'), 0, 0, tiled=True)  12.1 us
    ppermute x6, starting transfers between devices, flipped(): return lax.ppermute(x, ('wide', 'depth'), pairs)  6.81 us
    ppermute x6, waiting for transfers between devices, flipped(): return lax.ppermute(x, ('wide', 'depth'), pairs)  5.44 us
    pallas_call x1, Pallas kernels, shards(): pl.pallas_call(lambda *refs: attend_kernel((wide, narrow, halves, rows),...  3.17 us
    pallas_call x1, Pallas kernels, shards(): pl.pallas_call(lambda *refs: query_kernel((wide, halves, rows), *refs), o...  1.29 us
    unnamed x14, local copies, waits for them, and re-layouts  0.9 us
    pallas_call x1, Pallas kernels, shards(): pl.pallas_call(sum_kernel, out_shape=jax.ShapeDtypeStruct((rows, width //...  0.62 us
  transfers between devices with their start and end apart: 6, of which 5 were waited for; matrix products, arithmetic and copies ran while one was open for 0% of the time, Pallas kernels for 0%

profile of v3, /device:TPU:0, one launch (start us, length us, event | category | flops | bytes accessed | tf_op | source)
XLA Modules:
  0.0 30.5 jit_solution(11219783274503273645)
XLA Ops:
  0.0 0.0 copy-start.4
  0.0 0.0 copy-start.1
  0.0 0.0 copy-start.6
  0.0 0.9 %copy-done.6 = bf16[2,4096]{1,0:T(2,128)(2,1)S(1)} copy-done((bf16[2,4096]{1,0:T(2,128)(2,1)S(1)}, bf16[2,4096]{1,0:T(2,128)(2,1)}, u32[]{:S(2)}) %copy-start.6) | copy-done | bytes 16408
  0.9 0.0 copy-start
  0.9 0.1 shard_map.73
  1.0 0.0 copy-start.2
  1.0 0.0 copy-start.3
  1.0 0.0 copy-start.5
  1.1 3.1 %collective-permute-start.1 = (bf16[2,2048]{1,0:T(2,128)(2,1)S(1)}, bf16[2,2048]{1,0:T(2,128)(2,1)S(1)}, u32[]{:S(2)}, u32[]{:S(2)}) collective-permute-start(bf16[2,2048]{1,0:T(2,128)(2,1)S(1)} %get-tuple-element.11.refs_1_), channel_id=1, source_target_pairs={{0,16},{1,17},{8,24},{9,25},{16,0},{17,1},{24,8},{25,9},{2,18},{3,... | collective-permute-start | bytes 24584 | tf_op jit(solution)/shard_map/ppermute | solution.py:133
  4.1 1.4 %collective-permute-start.2 = (bf16[2,2048]{1,0:T(2,128)(2,1)S(1)}, bf16[2,2048]{1,0:T(2,128)(2,1)S(1)}, u32[]{:S(2)}, u32[]{:S(2)}) collective-permute-start(bf16[2,2048]{1,0:T(2,128)(2,1)S(1)} %get-tuple-element.12), channel_id=1, source_target_pairs={{0,17},{1,16},{8,25},{9,24},{16,1},{17,0},{24,9},{25,8},{2,19},{3,... | collective-permute-start | bytes 24584 | tf_op jit(solution)/shard_map/ppermute | solution.py:133
  5.6 0.1 collective-permute-start
  5.7 0.1 collective-permute-done.1.refs_3_
  5.7 2.9 %collective-permute-done.2.refs_4_ = bf16[2,2048]{1,0:T(2,128)(2,1)S(1)} collective-permute-done((bf16[2,2048]{1,0:T(2,128)(2,1)S(1)}, bf16[2,2048]{1,0:T(2,128)(2,1)S(1)}, u32[]{:S(2)}, u32[]{:S(2)}) %collective-permute-start.2) | collective-permute-done | bytes 8224 | tf_op jit(solution)/shard_map/ppermute | solution.py:133
  8.7 0.5 %collective-permute-done.refs_2_ = bf16[2,2048]{1,0:T(2,128)(2,1)S(1)} collective-permute-done((bf16[2,2048]{1,0:T(2,128)(2,1)S(1)}, bf16[2,2048]{1,0:T(2,128)(2,1)S(1)}, u32[]{:S(2)}, u32[]{:S(2)}) %collective-permute-start) | collective-permute-done | bytes 8224 | tf_op jit(solution)/shard_map/ppermute | solution.py:133
  9.2 0.0 copy-done.4
  9.2 0.0 copy-done.1
  9.2 1.3 %shard_map.74 = (f32[2,1024]{1,0:T(2,128)S(1)}, f32[2,1024]{1,0:T(2,128)S(1)}, f32[2,1024]{1,0:T(2,128)S(1)}, f32[2,1024]{1,0:T(2,128)S(1)}) custom-call(s32[16]{0:T(128)S(1)} %copy-done.4, bf16[2,2048]{1,0:T(2,128)(2,1)S(1)} %get-tuple-element.11.refs_1_, bf16[2,2048]{1,0:T(2,128)(2,1)S(1)} %collective-permute-done.refs_2_, ...), custom_call_target="tpu_custom_call" | custom-call | tf_op jit(solution)/shard_map/pallas_call | solution.py:153
  10.5 1.0 %collective-permute-start.3 = (f32[2,1024]{1,0:T(2,128)S(1)}, f32[2,1024]{1,0:T(2,128)S(1)}, u32[]{:S(2)}, u32[]{:S(2)}) collective-permute-start(f32[2,1024]{1,0:T(2,128)S(1)} %get-tuple-element.14), channel_id=1, source_target_pairs={{0,1},{1,0},{8,9},{9,8},{16,17},{17,16},{24,25},{25,24},{2,3},{3,2... | collective-permute-start | bytes 24584 | tf_op jit(solution)/shard_map/ppermute | solution.py:133
  11.5 0.0 collective-permute-start.4
  11.5 1.2 %collective-permute-start.5 = (f32[2,1024]{1,0:T(2,128)S(1)}, f32[2,1024]{1,0:T(2,128)S(1)}, u32[]{:S(2)}, u32[]{:S(2)}) collective-permute-start(f32[2,1024]{1,0:T(2,128)S(1)} %get-tuple-element.16), channel_id=1, source_target_pairs={{0,9},{1,8},{8,1},{9,0},{16,25},{17,24},{24,17},{25,16},{2,11},{3,... | collective-permute-start | bytes 24584 | tf_op jit(solution)/shard_map/ppermute | solution.py:133
  12.7 1.5 %collective-permute-done.3.refs_3_ = f32[2,1024]{1,0:T(2,128)S(1)} collective-permute-done((f32[2,1024]{1,0:T(2,128)S(1)}, f32[2,1024]{1,0:T(2,128)S(1)}, u32[]{:S(2)}, u32[]{:S(2)}) %collective-permute-start.3) | collective-permute-done | bytes 8224 | tf_op jit(solution)/shard_map/ppermute | solution.py:133
  14.2 0.0 collective-permute-done.4.refs_4_
  14.2 0.4 %collective-permute-done.5.refs_5_ = f32[2,1024]{1,0:T(2,128)S(1)} collective-permute-done((f32[2,1024]{1,0:T(2,128)S(1)}, f32[2,1024]{1,0:T(2,128)S(1)}, u32[]{:S(2)}, u32[]{:S(2)}) %collective-permute-start.5) | collective-permute-done | bytes 8224 | tf_op jit(solution)/shard_map/ppermute | solution.py:133
  14.6 0.0 copy-done
  14.6 0.0 copy-done.2
  14.6 0.0 copy-done.3
  14.6 0.0 copy-done.5
  14.6 3.2 %shard_map.75 = bf16[16,2,1024]{2,1,0:T(2,128)(2,1)S(1)} custom-call(s32[16]{0:T(128)S(1)} %copy-done.4, s32[16]{0:T(128)S(1)} %copy-done.5, f32[2,1024]{1,0:T(2,128)S(1)} %get-tuple-element.13.refs_2_, f32[2,1024]{1,0:T(2,128)S(1)} %collective-permute-done.3.refs_3_, f32[2,1024]{1,0:T(2,128)S(1)} %collective-permute-done.4.refs_4_, ...), custom_call_target="tpu_custom_call" | custom-call | tf_op jit(solution)/shard_map/pallas_call | solution.py:165
  17.8 12.1 %all_to_all.5.parts_ref = bf16[16,2,1024]{2,1,0:T(2,128)(2,1)S(1)} all-to-all(bf16[16,2,1024]{2,1,0:T(2,128)(2,1)S(1)} %shard_map.75), channel_id=1, replica_groups=mesh['wide'=4,'narrow'=4,'depth'=2] {'wide','narrow'}, dimensions={0} | all-to-all | bytes 131072 | tf_op jit(solution)/shard_map/all_to_all | solution.py:172
  29.9 0.6 %shard_map.76 = bf16[2,1024]{1,0:T(2,128)(2,1)} custom-call(bf16[16,2,1024]{2,1,0:T(2,128)(2,1)S(1)} %all_to_all.5.parts_ref), custom_call_target="tpu_custom_call" | custom-call | tf_op jit(solution)/shard_map/pallas_call | solution.py:173
Async XLA Ops:
  0.0 9.2 %copy-start.4 = (s32[16]{0:T(128)S(1)}, s32[16]{0:T(128)}, u32[]{:S(2)}) copy-start(s32[16]{0:T(128)} %refs_0_.3) | copy-start | bytes 196
  0.0 9.2 %copy-start.1 = (bf16[2048,1024]{1,0:T(8,128)(2,1)S(1)}, bf16[2048,1024]{1,0:T(8,128)(2,1)}, u32[]{:S(2)}) copy-start(bf16[2048,1024]{1,0:T(8,128)(2,1)} %refs_5_.1) | copy-start | bytes 12582916
  0.0 0.9 %copy-start.6 = (bf16[2,4096]{1,0:T(2,128)(2,1)S(1)}, bf16[2,4096]{1,0:T(2,128)(2,1)}, u32[]{:S(2)}) copy-start(bf16[2,4096]{1,0:T(2,128)(2,1)} %hidden_ref.1) | copy-start | bytes 49156
  0.9 13.7 %copy-start = (bf16[1024,4096]{1,0:T(8,128)(2,1)S(1)}, bf16[1024,4096]{1,0:T(8,128)(2,1)}, u32[]{:S(2)}) copy-start(bf16[1024,4096]{1,0:T(8,128)(2,1)} %refs_8_.1) | copy-start | bytes 25165828
  1.0 13.6 %copy-start.2 = (bf16[2,512,1024]{2,1,0:T(8,128)(2,1)S(1)}, bf16[2,512,1024]{2,1,0:T(8,128)(2,1)}, u32[]{:S(2)}) copy-start(bf16[2,512,1024]{2,1,0:T(8,128)(2,1)} %refs_6_.1) | copy-start | bytes 6291460
  1.0 13.6 %copy-start.3 = (bf16[2,512,1024]{2,1,0:T(8,128)(2,1)S(1)}, bf16[2,512,1024]{2,1,0:T(8,128)(2,1)}, u32[]{:S(2)}) copy-start(bf16[2,512,1024]{2,1,0:T(8,128)(2,1)} %refs_7_.1) | copy-start | bytes 6291460
  1.0 13.6 %copy-start.5 = (s32[16]{0:T(128)S(1)}, s32[16]{0:T(128)}, u32[]{:S(2)}) copy-start(s32[16]{0:T(128)} %refs_1_.1) | copy-start | bytes 196
  1.1 4.7 %collective-permute-start.1 = (bf16[2,2048]{1,0:T(2,128)(2,1)S(1)}, bf16[2,2048]{1,0:T(2,128)(2,1)S(1)}, u32[]{:S(2)}, u32[]{:S(2)}) collective-permute-start(bf16[2,2048]{1,0:T(2,128)(2,1)S(1)} %get-tuple-element.11.refs_1_), channel_id=1, source_target_pairs={{0,16},{1,17},{8,24},{9,25},{16,0},{17,1},{24,8},{25,9},{2,18},{3,... | collective-permute-start | bytes 24584 | tf_op jit(solution)/shard_map/ppermute | solution.py:133
  4.1 4.5 %collective-permute-start.2 = (bf16[2,2048]{1,0:T(2,128)(2,1)S(1)}, bf16[2,2048]{1,0:T(2,128)(2,1)S(1)}, u32[]{:S(2)}, u32[]{:S(2)}) collective-permute-start(bf16[2,2048]{1,0:T(2,128)(2,1)S(1)} %get-tuple-element.12), channel_id=1, source_target_pairs={{0,17},{1,16},{8,25},{9,24},{16,1},{17,0},{24,9},{25,8},{2,19},{3,... | collective-permute-start | bytes 24584 | tf_op jit(solution)/shard_map/ppermute | solution.py:133
  5.6 3.7 %collective-permute-start = (bf16[2,2048]{1,0:T(2,128)(2,1)S(1)}, bf16[2,2048]{1,0:T(2,128)(2,1)S(1)}, u32[]{:S(2)}, u32[]{:S(2)}) collective-permute-start(bf16[2,2048]{1,0:T(2,128)(2,1)S(1)} %get-tuple-element.12), channel_id=1, source_target_pairs={{0,1},{1,0},{8,9},{9,8},{16,17},{17,16},{24,25},{25,24},{2,3},{3,2... | collective-permute-start | bytes 24584 | tf_op jit(solution)/shard_map/ppermute | solution.py:133
  10.5 3.7 %collective-permute-start.3 = (f32[2,1024]{1,0:T(2,128)S(1)}, f32[2,1024]{1,0:T(2,128)S(1)}, u32[]{:S(2)}, u32[]{:S(2)}) collective-permute-start(f32[2,1024]{1,0:T(2,128)S(1)} %get-tuple-element.14), channel_id=1, source_target_pairs={{0,1},{1,0},{8,9},{9,8},{16,17},{17,16},{24,25},{25,24},{2,3},{3,2... | collective-permute-start | bytes 24584 | tf_op jit(solution)/shard_map/ppermute | solution.py:133
  11.5 2.7 %collective-permute-start.4 = (f32[2,1024]{1,0:T(2,128)S(1)}, f32[2,1024]{1,0:T(2,128)S(1)}, u32[]{:S(2)}, u32[]{:S(2)}) collective-permute-start(f32[2,1024]{1,0:T(2,128)S(1)} %get-tuple-element.15), channel_id=1, source_target_pairs={{0,8},{1,9},{8,0},{9,1},{16,24},{17,25},{24,16},{25,17},{2,10},{3,... | collective-permute-start | bytes 24584 | tf_op jit(solution)/shard_map/ppermute | solution.py:133
  11.5 3.1 %collective-permute-start.5 = (f32[2,1024]{1,0:T(2,128)S(1)}, f32[2,1024]{1,0:T(2,128)S(1)}, u32[]{:S(2)}, u32[]{:S(2)}) collective-permute-start(f32[2,1024]{1,0:T(2,128)S(1)} %get-tuple-element.16), channel_id=1, source_target_pairs={{0,9},{1,8},{8,1},{9,0},{16,25},{17,24},{24,17},{25,16},{2,11},{3,... | collective-permute-start | bytes 24584 | tf_op jit(solution)/shard_map/ppermute | solution.py:133

commit v4 on v3

--- a/solution.py
+++ b/solution.py
@@ -18,6 +18,10 @@
     for r in lead:
         found = jnp.where(slot_ref[r] == slot, jnp.int32(r), found)
     return found
+
+
+def crossing(chip, flip_depth):
+    return (chip & 1) ^ flip_depth
 
 
 def norm_kernel(hidden_ref, own_ref, other_ref):
@@ -53,7 +57,7 @@
             r = request_of(slot_ref, slot, range(total))
             from_wide = r // (rows * halves) ^ at_wide
             from_depth = (r // rows) % halves ^ at_depth
-            here = (from_wide & 1) == 0
+            here = (from_wide & 1) == crossing(from_wide >> 1, from_depth)
             place = ((from_wide >> 1) * halves + from_depth) * rows + r % rows
             row = sums_ref[pl.ds(place, 1), :]
             out[j : j + 1, :] = jnp.where(here, row, 0.0)
@@ -147,7 +151,8 @@
             if chip == 0 and flip_depth == 0:
                 pieces.append(own)
             else:
-                pieces.append(flipped(other if flip_depth else own, chip * 2, flip_depth))
+                flip_wide = chip * 2 + crossing(chip, flip_depth)
+                pieces.append(flipped(other if flip_depth else own, flip_wide, flip_depth))
     count = len(pieces) * rows
     sums = jax.ShapeDtypeStruct((rows, features), jnp.float32)
     parts = pl.pallas_call(

time: 30.7 us -> 29.8 us (0.971)
  blocking collectives: 12.1 us -> 11.6 us
  starting transfers between devices: 6.81 us -> 6.48 us
    all_to_all x1, blocking collectives: 12.1 us -> 11.6 us  [shards(): gathered = lax.all_to_all(spread, ('wide', 'narrow'), 0, 0, tiled=True)]
    ppermute x6, starting transfers between devices: 6.81 us -> 6.48 us  [flipped(): return lax.ppermute(x, ('wide', 'depth'), pairs)]
  transfers between devices with their start and end apart: 6 -> 6, of which waited for: 5 -> 4; matrix products, arithmetic and copies ran while one was open for 0% -> 0% of each run, Pallas kernels for 0% -> 0%
where the time goes in v4:
time: 29.8 us; the launch traced here: 29.5 us
  blocking collectives  11.6 us (39%)
  starting transfers between devices  6.48 us (22%)
  waiting for transfers between devices  5.26 us (18%)
  Pallas kernels  5.21 us (17%)
  local copies, waits for them, and re-layouts  0.9 us (3%)
    all_to_all x1, blocking collectives, shards(): gathered = lax.all_to_all(spread, ('wide', 'narrow'), 0, 0, tiled=True)  11.6 us
    ppermute x6, starting transfers between devices, flipped(): return lax.ppermute(x, ('wide', 'depth'), pairs)  6.48 us
    ppermute x6, waiting for transfers between devices, flipped(): return lax.ppermute(x, ('wide', 'depth'), pairs)  5.26 us
    pallas_call x1, Pallas kernels, shards(): pl.pallas_call(lambda *refs: attend_kernel((wide, narrow, halves, rows),...  3.17 us
    pallas_call x1, Pallas kernels, shards(): pl.pallas_call(lambda *refs: query_kernel((wide, halves, rows), *refs), o...  1.28 us
    unnamed x14, local copies, waits for them, and re-layouts  0.9 us
    pallas_call x1, Pallas kernels, shards(): pl.pallas_call(sum_kernel, out_shape=jax.ShapeDtypeStruct((rows, width //...  0.62 us
  transfers between devices with their start and end apart: 6, of which 4 were waited for; matrix products, arithmetic and copies ran while one was open for 0% of the time, Pallas kernels for 0%

profile of v4, /device:TPU:0, one launch (start us, length us, event | category | flops | bytes accessed | tf_op | source)
XLA Modules:
  0.0 29.5 jit_solution(7211867868037249780)
XLA Ops:
  0.0 0.0 copy-start.4
  0.0 0.0 copy-start.1
  0.0 0.0 copy-start.6
  0.0 0.9 %copy-done.6 = bf16[2,4096]{1,0:T(2,128)(2,1)S(1)} copy-done((bf16[2,4096]{1,0:T(2,128)(2,1)S(1)}, bf16[2,4096]{1,0:T(2,128)(2,1)}, u32[]{:S(2)}) %copy-start.6) | copy-done | bytes 16408
  0.9 0.0 copy-start
  0.9 0.1 shard_map.73
  1.0 0.0 copy-start.2
  1.0 0.0 copy-start.3
  1.0 0.0 copy-start.5
  1.1 2.5 %collective-permute-start.1 = (bf16[2,2048]{1,0:T(2,128)(2,1)S(1)}, bf16[2,2048]{1,0:T(2,128)(2,1)S(1)}, u32[]{:S(2)}, u32[]{:S(2)}) collective-permute-start(bf16[2,2048]{1,0:T(2,128)(2,1)S(1)} %get-tuple-element.11.refs_1_), channel_id=1, source_target_pairs={{0,24},{1,25},{8,16},{9,17},{16,8},{17,9},{24,0},{25,1},{2,26},{3,... | collective-permute-start | bytes 24584 | tf_op jit(solution)/shard_map/ppermute | solution.py:137
  3.6 1.6 %collective-permute-start.2 = (bf16[2,2048]{1,0:T(2,128)(2,1)S(1)}, bf16[2,2048]{1,0:T(2,128)(2,1)S(1)}, u32[]{:S(2)}, u32[]{:S(2)}) collective-permute-start(bf16[2,2048]{1,0:T(2,128)(2,1)S(1)} %get-tuple-element.12), channel_id=1, source_target_pairs={{0,17},{1,16},{8,25},{9,24},{16,1},{17,0},{24,9},{25,8},{2,19},{3,... | collective-permute-start | bytes 24584 | tf_op jit(solution)/shard_map/ppermute | solution.py:137
  5.1 0.2 collective-permute-start
  5.3 0.0 collective-permute-done.1.refs_3_
  5.3 2.8 %collective-permute-done.2.refs_4_ = bf16[2,2048]{1,0:T(2,128)(2,1)S(1)} collective-permute-done((bf16[2,2048]{1,0:T(2,128)(2,1)S(1)}, bf16[2,2048]{1,0:T(2,128)(2,1)S(1)}, u32[]{:S(2)}, u32[]{:S(2)}) %collective-permute-start.2) | collective-permute-done | bytes 8224 | tf_op jit(solution)/shard_map/ppermute | solution.py:137
  8.1 0.1 collective-permute-done.refs_2_
  8.2 0.0 copy-done.4
  8.2 0.0 copy-done.1
  8.2 1.3 %shard_map.74 = (f32[2,1024]{1,0:T(2,128)S(1)}, f32[2,1024]{1,0:T(2,128)S(1)}, f32[2,1024]{1,0:T(2,128)S(1)}, f32[2,1024]{1,0:T(2,128)S(1)}) custom-call(s32[16]{0:T(128)S(1)} %copy-done.4, bf16[2,2048]{1,0:T(2,128)(2,1)S(1)} %get-tuple-element.11.refs_1_, bf16[2,2048]{1,0:T(2,128)(2,1)S(1)} %collective-permute-done.refs_2_, ...), custom_call_target="tpu_custom_call" | custom-call | tf_op jit(solution)/shard_map/pallas_call | solution.py:158
  9.5 1.5 %collective-permute-start.3 = (f32[2,1024]{1,0:T(2,128)S(1)}, f32[2,1024]{1,0:T(2,128)S(1)}, u32[]{:S(2)}, u32[]{:S(2)}) collective-permute-start(f32[2,1024]{1,0:T(2,128)S(1)} %get-tuple-element.14), channel_id=1, source_target_pairs={{0,1},{1,0},{8,9},{9,8},{16,17},{17,16},{24,25},{25,24},{2,3},{3,2... | collective-permute-start | bytes 24584 | tf_op jit(solution)/shard_map/ppermute | solution.py:137
  11.0 0.0 collective-permute-start.4
  11.0 0.7 %collective-permute-start.5 = (f32[2,1024]{1,0:T(2,128)S(1)}, f32[2,1024]{1,0:T(2,128)S(1)}, u32[]{:S(2)}, u32[]{:S(2)}) collective-permute-start(f32[2,1024]{1,0:T(2,128)S(1)} %get-tuple-element.16), channel_id=1, source_target_pairs={{0,9},{1,8},{8,1},{9,0},{16,25},{17,24},{24,17},{25,16},{2,11},{3,... | collective-permute-start | bytes 24584 | tf_op jit(solution)/shard_map/ppermute | solution.py:137
  11.7 1.5 %collective-permute-done.3.refs_3_ = f32[2,1024]{1,0:T(2,128)S(1)} collective-permute-done((f32[2,1024]{1,0:T(2,128)S(1)}, f32[2,1024]{1,0:T(2,128)S(1)}, u32[]{:S(2)}, u32[]{:S(2)}) %collective-permute-start.3) | collective-permute-done | bytes 8224 | tf_op jit(solution)/shard_map/ppermute | solution.py:137
  13.2 0.0 collective-permute-done.4.refs_4_
  13.2 0.9 %collective-permute-done.5.refs_5_ = f32[2,1024]{1,0:T(2,128)S(1)} collective-permute-done((f32[2,1024]{1,0:T(2,128)S(1)}, f32[2,1024]{1,0:T(2,128)S(1)}, u32[]{:S(2)}, u32[]{:S(2)}) %collective-permute-start.5) | collective-permute-done | bytes 8224 | tf_op jit(solution)/shard_map/ppermute | solution.py:137
  14.1 0.0 copy-done
  14.1 0.0 copy-done.2
  14.1 0.0 copy-done.3
  14.1 0.0 copy-done.5
  14.1 3.2 %shard_map.75 = bf16[16,2,1024]{2,1,0:T(2,128)(2,1)S(1)} custom-call(s32[16]{0:T(128)S(1)} %copy-done.4, s32[16]{0:T(128)S(1)} %copy-done.5, f32[2,1024]{1,0:T(2,128)S(1)} %get-tuple-element.13.refs_2_, f32[2,1024]{1,0:T(2,128)S(1)} %collective-permute-done.3.refs_3_, f32[2,1024]{1,0:T(2,128)S(1)} %collective-permute-done.4.refs_4_, ...), custom_call_target="tpu_custom_call" | custom-call | tf_op jit(solution)/shard_map/pallas_call | solution.py:170
  17.3 11.6 %all_to_all.5.parts_ref = bf16[16,2,1024]{2,1,0:T(2,128)(2,1)S(1)} all-to-all(bf16[16,2,1024]{2,1,0:T(2,128)(2,1)S(1)} %shard_map.75), channel_id=1, replica_groups=mesh['wide'=4,'narrow'=4,'depth'=2] {'wide','narrow'}, dimensions={0} | all-to-all | bytes 131072 | tf_op jit(solution)/shard_map/all_to_all | solution.py:177
  28.9 0.6 %shard_map.76 = bf16[2,1024]{1,0:T(2,128)(2,1)} custom-call(bf16[16,2,1024]{2,1,0:T(2,128)(2,1)S(1)} %all_to_all.5.parts_ref), custom_call_target="tpu_custom_call" | custom-call | tf_op jit(solution)/shard_map/pallas_call | solution.py:178
Async XLA Ops:
  0.0 8.2 %copy-start.4 = (s32[16]{0:T(128)S(1)}, s32[16]{0:T(128)}, u32[]{:S(2)}) copy-start(s32[16]{0:T(128)} %refs_0_.3) | copy-start | bytes 196
  0.0 8.2 %copy-start.1 = (bf16[2048,1024]{1,0:T(8,128)(2,1)S(1)}, bf16[2048,1024]{1,0:T(8,128)(2,1)}, u32[]{:S(2)}) copy-start(bf16[2048,1024]{1,0:T(8,128)(2,1)} %refs_5_.1) | copy-start | bytes 12582916
  0.0 0.9 %copy-start.6 = (bf16[2,4096]{1,0:T(2,128)(2,1)S(1)}, bf16[2,4096]{1,0:T(2,128)(2,1)}, u32[]{:S(2)}) copy-start(bf16[2,4096]{1,0:T(2,128)(2,1)} %hidden_ref.1) | copy-start | bytes 49156
  0.9 13.2 %copy-start = (bf16[1024,4096]{1,0:T(8,128)(2,1)S(1)}, bf16[1024,4096]{1,0:T(8,128)(2,1)}, u32[]{:S(2)}) copy-start(bf16[1024,4096]{1,0:T(8,128)(2,1)} %refs_8_.1) | copy-start | bytes 25165828
  1.0 13.1 %copy-start.2 = (bf16[2,512,1024]{2,1,0:T(8,128)(2,1)S(1)}, bf16[2,512,1024]{2,1,0:T(8,128)(2,1)}, u32[]{:S(2)}) copy-start(bf16[2,512,1024]{2,1,0:T(8,128)(2,1)} %refs_6_.1) | copy-start | bytes 6291460
  1.0 13.1 %copy-start.3 = (bf16[2,512,1024]{2,1,0:T(8,128)(2,1)S(1)}, bf16[2,512,1024]{2,1,0:T(8,128)(2,1)}, u32[]{:S(2)}) copy-start(bf16[2,512,1024]{2,1,0:T(8,128)(2,1)} %refs_7_.1) | copy-start | bytes 6291460
  1.0 13.1 %copy-start.5 = (s32[16]{0:T(128)S(1)}, s32[16]{0:T(128)}, u32[]{:S(2)}) copy-start(s32[16]{0:T(128)} %refs_1_.1) | copy-start | bytes 196
  1.1 4.3 %collective-permute-start.1 = (bf16[2,2048]{1,0:T(2,128)(2,1)S(1)}, bf16[2,2048]{1,0:T(2,128)(2,1)S(1)}, u32[]{:S(2)}, u32[]{:S(2)}) collective-permute-start(bf16[2,2048]{1,0:T(2,128)(2,1)S(1)} %get-tuple-element.11.refs_1_), channel_id=1, source_target_pairs={{0,24},{1,25},{8,16},{9,17},{16,8},{17,9},{24,0},{25,1},{2,26},{3,... | collective-permute-start | bytes 24584 | tf_op jit(solution)/shard_map/ppermute | solution.py:137
  3.6 4.5 %collective-permute-start.2 = (bf16[2,2048]{1,0:T(2,128)(2,1)S(1)}, bf16[2,2048]{1,0:T(2,128)(2,1)S(1)}, u32[]{:S(2)}, u32[]{:S(2)}) collective-permute-start(bf16[2,2048]{1,0:T(2,128)(2,1)S(1)} %get-tuple-element.12), channel_id=1, source_target_pairs={{0,17},{1,16},{8,25},{9,24},{16,1},{17,0},{24,9},{25,8},{2,19},{3,... | collective-permute-start | bytes 24584 | tf_op jit(solution)/shard_map/ppermute | solution.py:137
  5.1 3.1 %collective-permute-start = (bf16[2,2048]{1,0:T(2,128)(2,1)S(1)}, bf16[2,2048]{1,0:T(2,128)(2,1)S(1)}, u32[]{:S(2)}, u32[]{:S(2)}) collective-permute-start(bf16[2,2048]{1,0:T(2,128)(2,1)S(1)} %get-tuple-element.12), channel_id=1, source_target_pairs={{0,9},{1,8},{8,1},{9,0},{16,25},{17,24},{24,17},{25,16},{2,11},{3,... | collective-permute-start | bytes 24584 | tf_op jit(solution)/shard_map/ppermute | solution.py:137
  9.5 3.7 %collective-permute-start.3 = (f32[2,1024]{1,0:T(2,128)S(1)}, f32[2,1024]{1,0:T(2,128)S(1)}, u32[]{:S(2)}, u32[]{:S(2)}) collective-permute-start(f32[2,1024]{1,0:T(2,128)S(1)} %get-tuple-element.14), channel_id=1, source_target_pairs={{0,1},{1,0},{8,9},{9,8},{16,17},{17,16},{24,25},{25,24},{2,3},{3,2... | collective-permute-start | bytes 24584 | tf_op jit(solution)/shard_map/ppermute | solution.py:137
  11.0 2.2 %collective-permute-start.4 = (f32[2,1024]{1,0:T(2,128)S(1)}, f32[2,1024]{1,0:T(2,128)S(1)}, u32[]{:S(2)}, u32[]{:S(2)}) collective-permute-start(f32[2,1024]{1,0:T(2,128)S(1)} %get-tuple-element.15), channel_id=1, source_target_pairs={{0,8},{1,9},{8,0},{9,1},{16,24},{17,25},{24,16},{25,17},{2,10},{3,... | collective-permute-start | bytes 24584 | tf_op jit(solution)/shard_map/ppermute | solution.py:137
  11.0 3.1 %collective-permute-start.5 = (f32[2,1024]{1,0:T(2,128)S(1)}, f32[2,1024]{1,0:T(2,128)S(1)}, u32[]{:S(2)}, u32[]{:S(2)}) collective-permute-start(f32[2,1024]{1,0:T(2,128)S(1)} %get-tuple-element.16), channel_id=1, source_target_pairs={{0,9},{1,8},{8,1},{9,0},{16,25},{17,24},{24,17},{25,16},{2,11},{3,... | collective-permute-start | bytes 24584 | tf_op jit(solution)/shard_map/ppermute | solution.py:137

commit v5 on v0

v5 whole, which is shorter than its diff:
```python
import jax
import jax.numpy as jnp
from jax import lax
from jax.experimental import pallas as pl
from jax.experimental.pallas import tpu as pltpu
from jax.sharding import PartitionSpec as P

HDIM = 64
BLOCK = 128
SUBLANES = 8
LANES = 128

MIB = 1 << 20
VMEM = pl.BlockSpec(memory_space=pltpu.VMEM)


def crossing(chip, flip_depth):
    return (chip & 1) ^ flip_depth


def table_kernel(sizes, slot_ref, blocks_ref, place_ref, limit_ref, route_ref):
    wide, halves, rows = sizes
    at_wide, at_depth = lax.axis_index("wide"), lax.axis_index("depth")
    total = slot_ref.shape[1]
    slots = slot_ref[...]

    def iota(count, dim):
        return lax.broadcasted_iota(jnp.int32, (count, total), dim)

    target = iota(SUBLANES, 0)
    peer = target // rows
    slot = ((at_wide ^ (peer // 2)) * halves + (at_depth ^ (peer % 2))) * rows + target % rows
    request = jnp.sum(jnp.where(slots == slot, iota(SUBLANES, 1), 0), axis=1, keepdims=True)
    from_wide = (request // (rows * halves)) ^ at_wide
    from_depth = (request // rows % halves) ^ at_depth
    place = ((from_wide >> 1) * halves + from_depth) * rows + request % rows
    here = (from_wide & 1) == crossing(from_wide >> 1, from_depth)
    place_ref[...] = jnp.broadcast_to(jnp.where(here, place, -1), place_ref.shape)
    base = (at_wide * halves + at_depth) * rows
    for j in range(rows):
        count = jnp.sum(jnp.where(slots == base + j, blocks_ref[...], 0), axis=1, keepdims=True)
        limit_ref[j] = jnp.broadcast_to(count * BLOCK, limit_ref.shape[1:])
    line = iota(wide * rows, 0)
    request = (line // rows * halves + at_depth) * rows + line % rows
    held = jnp.sum(jnp.where(iota(wide * rows, 1) == request, slots, 0), axis=1, keepdims=True)
    route_ref[...] = jnp.broadcast_to(held - base, route_ref.shape)


def query_kernel(rows, place_ref, *refs):
    pieces = len(refs) - 1 - 4 - 1
    piece_refs, weight_ref = refs[:pieces], refs[pieces]
    out_refs, rows_ref = refs[pieces + 1 : pieces + 5], refs[pieces + 5]
    half = weight_ref.shape[0]
    at_depth = lax.axis_index("depth")
    for k, piece in enumerate(piece_refs):
        rows_ref[k * rows : (k + 1) * rows, :] = piece[...].astype(jnp.float32)
    widened = rows_ref[...]
    mean_square = jnp.mean(widened * widened, axis=-1, keepdims=True)
    used = rows_ref[:, pl.ds(pl.multiple_of(at_depth * half, LANES), half)]
    normed = (used * lax.rsqrt(mean_square + 1e-06)).astype(jnp.bfloat16)
    sums = jnp.dot(normed, weight_ref[...], preferred_element_type=jnp.float32)
    place = place_ref[...]
    for c in range(sums.shape[1] // LANES):
        span = slice(c * LANES, (c + 1) * LANES)
        picked = jnp.zeros_like(place, jnp.float32)
        for g in range(sums.shape[0] // SUBLANES):
            lines = sums[g * SUBLANES : (g + 1) * SUBLANES, span]
            found = jnp.take_along_axis(lines, place & (SUBLANES - 1), axis=0)
            picked = jnp.where(place >> 3 == g, found, picked)
        for k, out in enumerate(out_refs):
            out[:, span] = picked[k * rows : (k + 1) * rows]


def attend_kernel(narrow, limit_ref, route_ref, *refs):
    parts, (keys_ref, values_ref, weight_ref, out_ref) = refs[:4], refs[4:]
    rows, cache_len, features = keys_ref.shape
    heads = features // HDIM
    queries = (parts[0][...] + parts[2][...]) + (parts[1][...] + parts[3][...])
    of_head = (
        lax.broadcasted_iota(jnp.int32, (heads, features), 1) // HDIM
        == lax.broadcasted_iota(jnp.int32, (heads, features), 0)
    )
    positions = lax.broadcasted_iota(jnp.int32, (heads, cache_len), 1)
    scores, shares, mixed = [], [], []
    for j in range(rows):
        spread = jnp.where(of_head, queries[j : j + 1, :], 0.0).astype(jnp.bfloat16)
        scores.append(
            lax.dot_general(
                spread, keys_ref[j], (((1,), (1,)), ((), ())), preferred_element_type=jnp.float32
            )
        )
    for j in range(rows):
        masked = jnp.where(positions < limit_ref[j], scores[j], jnp.float32(-1e30))
        row_top = jnp.max(masked, axis=-1, keepdims=True)
        raised = jnp.exp(masked - row_top)
        shares.append((raised / jnp.sum(raised, axis=-1, keepdims=True)).astype(jnp.bfloat16))
    for j in range(rows):
        mixed.append(jnp.dot(shares[j], values_ref[j], preferred_element_type=jnp.float32))
    route = route_ref[...]
    context = jnp.zeros(route.shape, jnp.float32)
    for j in range(rows):
        line = jnp.sum(jnp.where(of_head, mixed[j], 0.0), axis=0, keepdims=True)
        context = jnp.where(route == j, line, context)
    partial = jnp.dot(
        context.astype(jnp.bfloat16), weight_ref[...], preferred_element_type=jnp.float32
    )
    width = partial.shape[1] // narrow
    for to_wide in range(partial.shape[0] // rows):
        block = partial[to_wide * rows : (to_wide + 1) * rows].astype(jnp.bfloat16)
        for to_narrow in range(narrow):
            out_ref[to_wide * narrow + to_narrow] = block[
                :, to_narrow * width : (to_narrow + 1) * width
            ]


def sum_kernel(parts_ref, out_ref):
    total = parts_ref[0].astype(jnp.float32)
    for k in range(1, parts_ref.shape[0]):
        total = total + parts_ref[k].astype(jnp.float32)
    out_ref[...] = total.astype(jnp.bfloat16)


def local_call(kernel, out_shape, count, mib, scratch=(), cost=None):
    several = isinstance(out_shape, list)
    return pl.pallas_call(
        kernel,
        out_shape=out_shape,
        in_specs=[VMEM] * count,
        out_specs=[VMEM] * len(out_shape) if several else VMEM,
        scratch_shapes=scratch,
        compiler_params=pltpu.CompilerParams(vmem_limit_bytes=mib * MIB),
        cost_estimate=cost,
    )


def shards(
    hidden_state, query_weight, output_weight, cache_keys, cache_values, enc_blocks, cache_slot
):
    rows, model = hidden_state.shape
    wide, narrow, halves = (lax.axis_size(name) for name in ("wide", "narrow", "depth"))
    features = query_weight.shape[1]
    cache_len = cache_keys.shape[1]
    width = output_weight.shape[1]

    def flipped(x, flip_wide, flip_depth):
        pairs = [
            (w * halves + d, (w ^ flip_wide) * halves + (d ^ flip_depth))
            for w in range(wide)
            for d in range(halves)
        ]
        return lax.ppermute(x, ("wide", "depth"), pairs)

    shape = jax.ShapeDtypeStruct
    place, limit, route = local_call(
        lambda *refs: table_kernel((wide, halves, rows), *refs),
        [
            shape((4 * rows, LANES), jnp.int32),
            shape((rows, features // HDIM, cache_len), jnp.int32),
            shape((wide * rows, features), jnp.int32),
        ],
        2,
        1,
        cost=pl.CostEstimate(flops=10**10, bytes_accessed=0, transcendentals=0),
    )(cache_slot[None], enc_blocks[None])
    pieces = []
    for chip in range(wide // 2):
        for flip_depth in range(halves):
            if chip == 0 and flip_depth == 0:
                pieces.append(hidden_state)
            else:
                flip_wide = chip * 2 + crossing(chip, flip_depth)
                pieces.append(flipped(hidden_state, flip_wide, flip_depth))
    parts = local_call(
        lambda *refs: query_kernel(rows, *refs),
        [shape((rows, features), jnp.float32)] * 4,
        len(pieces) + 2,
        6,
        scratch=[pltpu.VMEM((len(pieces) * rows, model), jnp.float32)],
    )(place, *pieces, query_weight)
    arrived = [parts[0]] + [flipped(parts[k], k // 2, k % 2) for k in range(1, 4)]
    spread = local_call(
        lambda *refs: attend_kernel(narrow, *refs),
        shape((wide * narrow, rows, width // narrow), jnp.bfloat16),
        9,
        16,
    )(limit, route, *arrived, cache_keys, cache_values, output_weight)
    gathered = lax.all_to_all(spread, ("wide", "narrow"), 0, 0, tiled=True)
    return local_call(
        sum_kernel, shape((rows, width // narrow), jnp.bfloat16), 1, 1
    )(gathered)


def solution(mesh):
    placed = (
        P(("wide", "depth"), None),
        P("depth", "narrow"),
        P("narrow", None),
        P(("wide", "depth"), None, "narrow"),
        P(("wide", "depth"), None, "narrow"),
        P(),
        P(),
    )
    return jax.shard_map(
        shards,
        mesh=mesh,
        in_specs=placed,
        out_specs=P(("wide", "depth"), "narrow"),
        check_vma=False,
    )
```

time: 117 us -> 29.3 us (0.25)
  waiting for transfers between devices: 43.2 us -> 4.92 us
  blocking collectives: 30.7 us -> 12.5 us
  between operations: 14.8 us -> 0.07 us
  matrix products: 14 us -> 0 us
  local copies, waits for them, and re-layouts: 12 us -> 1.66 us
  starting transfers between devices: 0.01 us -> 6.36 us
  Pallas kernels: 0 us -> 3.68 us
  other arithmetic: 1.82 us -> 0.01 us
    unnamed x2 -> x0, waiting for transfers between devices: 43.2 us -> none
    unnamed x2 -> x0, blocking collectives: 20.2 us -> none
    all_to_all x0 -> x1, blocking collectives: none -> 12.5 us  [shards(): gathered = lax.all_to_all(spread, ('wide', 'narrow'), 0, 0, tiled=True)]
    all_gather x2 -> x0, blocking collectives: 10.5 us -> none  [the longest x1 5.33 us: shards(): lax.all_gather(normed, 'depth', axis=0, tiled=True)]
    unnamed x11 -> x16, local copies, waits for them, and re-layouts: 9.86 us -> 1.66 us
    unnamed x1 -> x0, matrix products: 8.1 us -> none
    ppermute x0 -> x6, starting transfers between devices: none -> 6.36 us  [flipped(): return lax.ppermute(x, ('wide', 'depth'), pairs)]
    ppermute x0 -> x6, waiting for transfers between devices: none -> 4.92 us  [flipped(): return lax.ppermute(x, ('wide', 'depth'), pairs)]
  transfers between devices with their start and end apart: 1 -> 6, of which waited for: 1 -> 3; matrix products, arithmetic and copies ran while one was open for 0% -> 0% of each run, Pallas kernels for 0% -> 0%
where the time goes in v5:
time: 29.3 us; the launch traced here: 29.2 us
  blocking collectives  12.5 us (43%)
  starting transfers between devices  6.36 us (22%)
  waiting for transfers between devices  4.92 us (17%)
  Pallas kernels  3.68 us (13%)
  local copies, waits for them, and re-layouts  1.66 us (6%)
    all_to_all x1, blocking collectives, shards(): gathered = lax.all_to_all(spread, ('wide', 'narrow'), 0, 0, tiled=True)  12.5 us
    ppermute x6, starting transfers between devices, flipped(): return lax.ppermute(x, ('wide', 'depth'), pairs)  6.36 us
    ppermute x6, waiting for transfers between devices, flipped(): return lax.ppermute(x, ('wide', 'depth'), pairs)  4.92 us
    pallas_call x1, Pallas kernels, shards(): local_call(lambda *refs: attend_kernel(narrow, *refs), shape((wide * narr...  2.16 us
    unnamed x16, local copies, waits for them, and re-layouts  1.66 us
    pallas_call x1, Pallas kernels, shards(): local_call(lambda *refs: query_kernel(rows, *refs), [shape((rows, feature...  0.79 us
    pallas_call x1, Pallas kernels, shards(): local_call(sum_kernel, shape((rows, width // narrow), jnp.bfloat16), 1, 1)  0.62 us
  transfers between devices with their start and end apart: 6, of which 3 were waited for; matrix products, arithmetic and copies ran while one was open for 0% of the time, Pallas kernels for 0%

profile of v5, /device:TPU:0, one launch (start us, length us, event | category | flops | bytes accessed | tf_op | source)
XLA Modules:
  0.0 29.2 jit_solution(13781790101391103726)
XLA Ops:
  0.0 2.4 %collective-permute-start.1 = (bf16[2,4096]{1,0:T(2,128)(2,1)}, bf16[2,4096]{1,0:T(2,128)(2,1)S(1)}, u32[]{:S(2)}, u32[]{:S(2)}) collective-permute-start(bf16[2,4096]{1,0:T(2,128)(2,1)} %refs_1_.1), channel_id=1, source_target_pairs={{0,24},{1,25},{8,16},{9,17},{16,8},{17,9},{24,0},{25,1},{2,26},{3,... | collective-permute-start | bytes 49160 | tf_op jit(solution)/shard_map/ppermute | solution.py:151
  2.4 1.8 %collective-permute-start = (bf16[2,4096]{1,0:T(2,128)(2,1)}, bf16[2,4096]{1,0:T(2,128)(2,1)S(1)}, u32[]{:S(2)}, u32[]{:S(2)}) collective-permute-start(bf16[2,4096]{1,0:T(2,128)(2,1)} %refs_1_.1), channel_id=1, source_target_pairs={{0,9},{1,8},{8,1},{9,0},{16,25},{17,24},{24,17},{25,16},{2,11},{3,... | collective-permute-start | bytes 49160 | tf_op jit(solution)/shard_map/ppermute | solution.py:151
  4.2 0.0 collective-permute-start.2
  4.2 0.0 slice-start
  4.2 0.0 copy-start.4
  4.2 0.8 %copy-done.4 = s32[16]{0:T(128)S(1)} copy-done((s32[16]{0:T(128)S(1)}, s32[16]{0:T(128)}, u32[]{:S(2)}) %copy-start.4) | copy-done | bytes 88
  5.0 0.0 copy-start.5
  5.0 0.8 %copy-done.5 = s32[16]{0:T(128)S(1)} copy-done((s32[16]{0:T(128)S(1)}, s32[16]{0:T(128)}, u32[]{:S(2)}) %copy-start.5) | copy-done | bytes 88
  5.8 0.0 copy-start
  5.8 0.0 copy-start.3
  5.8 0.1 shard_map.73
  6.0 0.0 copy-start.1
  6.0 0.0 copy-start.2
  6.0 0.0 collective-permute-done.1.refs_3_
  6.0 0.0 collective-permute-done.refs_2_
  6.0 3.0 %collective-permute-done.2.refs_4_ = bf16[2,4096]{1,0:T(2,128)(2,1)S(1)} collective-permute-done((bf16[2,4096]{1,0:T(2,128)(2,1)}, bf16[2,4096]{1,0:T(2,128)(2,1)S(1)}, u32[]{:S(2)}, u32[]{:S(2)}) %collective-permute-start.2) | collective-permute-done | bytes 16416 | tf_op jit(solution)/shard_map/ppermute | solution.py:151
  9.1 0.0 copy-done
  9.1 0.0 copy-done.3
  9.1 0.8 %shard_map.74 = (f32[2,1024]{1,0:T(2,128)S(1)}, f32[2,1024]{1,0:T(2,128)S(1)}, f32[2,1024]{1,0:T(2,128)S(1)}, f32[2,1024]{1,0:T(2,128)S(1)}) custom-call(s32[8,128]{1,0:T(8,128)S(1)} %get-tuple-element.14.refs_0_, bf16[2,4096]{1,0:T(2,128)(2,1)S(1)} %copy-done.3, bf16[2,4096]{1,0:T(2,128)(2,1)S(1)} %collective-permute-done.refs_2_, ...), custom_call_target="tpu_custom_call" | custom-call | tf_op jit(solution)/shard_map/pallas_call | solution.py:173
  9.9 0.9 %collective-permute-start.3 = (f32[2,1024]{1,0:T(2,128)S(1)}, f32[2,1024]{1,0:T(2,128)S(1)}, u32[]{:S(2)}, u32[]{:S(2)}) collective-permute-start(f32[2,1024]{1,0:T(2,128)S(1)} %get-tuple-element.16), channel_id=1, source_target_pairs={{0,1},{1,0},{8,9},{9,8},{16,17},{17,16},{24,25},{25,24},{2,3},{3,2... | collective-permute-start | bytes 24584 | tf_op jit(solution)/shard_map/ppermute | solution.py:151
  10.8 0.0 collective-permute-start.4
  10.8 1.2 %collective-permute-start.5 = (f32[2,1024]{1,0:T(2,128)S(1)}, f32[2,1024]{1,0:T(2,128)S(1)}, u32[]{:S(2)}, u32[]{:S(2)}) collective-permute-start(f32[2,1024]{1,0:T(2,128)S(1)} %get-tuple-element.18), channel_id=1, source_target_pairs={{0,9},{1,8},{8,1},{9,0},{16,25},{17,24},{24,17},{25,16},{2,11},{3,... | collective-permute-start | bytes 24584 | tf_op jit(solution)/shard_map/ppermute | solution.py:151
  12.0 1.5 %collective-permute-done.3.refs_3_ = f32[2,1024]{1,0:T(2,128)S(1)} collective-permute-done((f32[2,1024]{1,0:T(2,128)S(1)}, f32[2,1024]{1,0:T(2,128)S(1)}, u32[]{:S(2)}, u32[]{:S(2)}) %collective-permute-start.3) | collective-permute-done | bytes 8224 | tf_op jit(solution)/shard_map/ppermute | solution.py:151
  13.5 0.0 collective-permute-done.4.refs_4_
  13.5 0.4 %collective-permute-done.5.refs_5_ = f32[2,1024]{1,0:T(2,128)S(1)} collective-permute-done((f32[2,1024]{1,0:T(2,128)S(1)}, f32[2,1024]{1,0:T(2,128)S(1)}, u32[]{:S(2)}, u32[]{:S(2)}) %collective-permute-start.5) | collective-permute-done | bytes 8224 | tf_op jit(solution)/shard_map/ppermute | solution.py:151
  13.9 0.0 slice-done
  13.9 0.0 slice-done.1
  13.9 0.0 copy-done.1
  13.9 0.0 copy-done.2
  13.9 2.2 %shard_map.75 = bf16[16,2,1024]{2,1,0:T(2,128)(2,1)S(1)} custom-call(s32[2,16,512]{2,1,0:T(8,128)S(1)} %get-tuple-element.12.refs_0_, s32[8,1024]{1,0:T(8,128)S(1)} %get-tuple-element.13.refs_1_, f32[2,1024]{1,0:T(2,128)S(1)} %get-tuple-element.15.refs_2_, f32[2,1024]{1,0:T(2,128)S(1)} %collective-permute-done.3.refs_3_, ...), custom_call_target="tpu_custom_call" | custom-call | tf_op jit(solution)/shard_map/pallas_call | solution.py:181
  16.1 12.5 %all_to_all.5.parts_ref = bf16[16,2,1024]{2,1,0:T(2,128)(2,1)S(1)} all-to-all(bf16[16,2,1024]{2,1,0:T(2,128)(2,1)S(1)} %shard_map.75), channel_id=1, replica_groups=mesh['wide'=4,'narrow'=4,'depth'=2] {'wide','narrow'}, dimensions={0} | all-to-all | bytes 131072 | tf_op jit(solution)/shard_map/all_to_all | solution.py:187
  28.5 0.6 %shard_map.76 = bf16[2,1024]{1,0:T(2,128)(2,1)} custom-call(bf16[16,2,1024]{2,1,0:T(2,128)(2,1)S(1)} %all_to_all.5.parts_ref), custom_call_target="tpu_custom_call" | custom-call | tf_op jit(solution)/shard_map/pallas_call | solution.py:188
  (2 shorter events, 0.0 us)
Async XLA Ops:
  0.0 6.0 %collective-permute-start.1 = (bf16[2,4096]{1,0:T(2,128)(2,1)}, bf16[2,4096]{1,0:T(2,128)(2,1)S(1)}, u32[]{:S(2)}, u32[]{:S(2)}) collective-permute-start(bf16[2,4096]{1,0:T(2,128)(2,1)} %refs_1_.1), channel_id=1, source_target_pairs={{0,24},{1,25},{8,16},{9,17},{16,8},{17,9},{24,0},{25,1},{2,26},{3,... | collective-permute-start | bytes 49160 | tf_op jit(solution)/shard_map/ppermute | solution.py:151
  2.4 3.6 %collective-permute-start = (bf16[2,4096]{1,0:T(2,128)(2,1)}, bf16[2,4096]{1,0:T(2,128)(2,1)S(1)}, u32[]{:S(2)}, u32[]{:S(2)}) collective-permute-start(bf16[2,4096]{1,0:T(2,128)(2,1)} %refs_1_.1), channel_id=1, source_target_pairs={{0,9},{1,8},{8,1},{9,0},{16,25},{17,24},{24,17},{25,16},{2,11},{3,... | collective-permute-start | bytes 49160 | tf_op jit(solution)/shard_map/ppermute | solution.py:151
  4.2 4.8 %collective-permute-start.2 = (bf16[2,4096]{1,0:T(2,128)(2,1)}, bf16[2,4096]{1,0:T(2,128)(2,1)S(1)}, u32[]{:S(2)}, u32[]{:S(2)}) collective-permute-start(bf16[2,4096]{1,0:T(2,128)(2,1)} %refs_1_.1), channel_id=1, source_target_pairs={{0,17},{1,16},{8,25},{9,24},{16,1},{17,0},{24,9},{25,8},{2,19},{3,... | collective-permute-start | bytes 49160 | tf_op jit(solution)/shard_map/ppermute | solution.py:151
  4.2 9.7 %slice-start = ((s8[8388608]{0:T(1024)(128)(4,1)}), s8[4194304]{0:T(1024)(128)(4,1)S(1)}, s32[]{:S(2)}) async-start(s8[8388608]{0:T(1024)(128)(4,1)} %bitcast.2), calls=%async_computation.1 | async-start | bytes 8388608
  4.2 0.8 %copy-start.4 = (s32[16]{0:T(128)S(1)}, s32[16]{0:T(128)}, u32[]{:S(2)}) copy-start(s32[16]{0:T(128)} %param.13) | copy-start | bytes 196
  5.0 0.8 %copy-start.5 = (s32[16]{0:T(128)S(1)}, s32[16]{0:T(128)}, u32[]{:S(2)}) copy-start(s32[16]{0:T(128)} %param.12) | copy-start | bytes 196
  5.8 3.2 %copy-start = (bf16[2048,1024]{1,0:T(8,128)(2,1)S(1)}, bf16[2048,1024]{1,0:T(8,128)(2,1)}, u32[]{:S(2)}) copy-start(bf16[2048,1024]{1,0:T(8,128)(2,1)} %refs_5_.1) | copy-start | bytes 12582916
  5.8 3.2 %copy-start.3 = (bf16[2,4096]{1,0:T(2,128)(2,1)S(1)}, bf16[2,4096]{1,0:T(2,128)(2,1)}, u32[]{:S(2)}) copy-start(bf16[2,4096]{1,0:T(2,128)(2,1)} %refs_1_.1) | copy-start | bytes 49156
  5.8 8.0 %slice-start.1 = ((s8[8388608]{0:T(1024)(128)(4,1)}), s8[4194304]{0:T(1024)(128)(4,1)S(1)}, s32[]{:S(2)}) async-start(s8[8388608]{0:T(1024)(128)(4,1)} %bitcast.2), calls=%async_computation.2 | async-start | bytes 8388608
  6.0 7.9 %copy-start.1 = (bf16[2,512,1024]{2,1,0:T(8,128)(2,1)S(1)}, bf16[2,512,1024]{2,1,0:T(8,128)(2,1)}, u32[]{:S(2)}) copy-start(bf16[2,512,1024]{2,1,0:T(8,128)(2,1)} %refs_6_.1) | copy-start | bytes 6291460
  6.0 7.9 %copy-start.2 = (bf16[2,512,1024]{2,1,0:T(8,128)(2,1)S(1)}, bf16[2,512,1024]{2,1,0:T(8,128)(2,1)}, u32[]{:S(2)}) copy-start(bf16[2,512,1024]{2,1,0:T(8,128)(2,1)} %refs_7_.1) | copy-start | bytes 6291460
  9.9 3.7 %collective-permute-start.3 = (f32[2,1024]{1,0:T(2,128)S(1)}, f32[2,1024]{1,0:T(2,128)S(1)}, u32[]{:S(2)}, u32[]{:S(2)}) collective-permute-start(f32[2,1024]{1,0:T(2,128)S(1)} %get-tuple-element.16), channel_id=1, source_target_pairs={{0,1},{1,0},{8,9},{9,8},{16,17},{17,16},{24,25},{25,24},{2,3},{3,2... | collective-permute-start | bytes 24584 | tf_op jit(solution)/shard_map/ppermute | solution.py:151
  10.8 2.7 %collective-permute-start.4 = (f32[2,1024]{1,0:T(2,128)S(1)}, f32[2,1024]{1,0:T(2,128)S(1)}, u32[]{:S(2)}, u32[]{:S(2)}) collective-permute-start(f32[2,1024]{1,0:T(2,128)S(1)} %get-tuple-element.17), channel_id=1, source_target_pairs={{0,8},{1,9},{8,0},{9,1},{16,24},{17,25},{24,16},{25,17},{2,10},{3,... | collective-permute-start | bytes 24584 | tf_op jit(solution)/shard_map/ppermute | solution.py:151
  10.8 3.1 %collective-permute-start.5 = (f32[2,1024]{1,0:T(2,128)S(1)}, f32[2,1024]{1,0:T(2,128)S(1)}, u32[]{:S(2)}, u32[]{:S(2)}) collective-permute-start(f32[2,1024]{1,0:T(2,128)S(1)} %get-tuple-element.18), channel_id=1, source_target_pairs={{0,9},{1,8},{8,1},{9,0},{16,25},{17,24},{24,17},{25,16},{2,11},{3,... | collective-permute-start | bytes 24584 | tf_op jit(solution)/shard_map/ppermute | solution.py:151

commit v6 on v5

--- a/solution.py
+++ b/solution.py
@@ -18,8 +18,27 @@
     return (chip & 1) ^ flip_depth
 
 
-def table_kernel(sizes, slot_ref, blocks_ref, place_ref, limit_ref, route_ref):
+def norm_kernel(hidden_ref, own_ref, other_ref):
+    half = own_ref.shape[1]
+    at_depth = lax.axis_index("depth")
+    widened = hidden_ref[...].astype(jnp.float32)
+    mean_square = jnp.mean(widened * widened, axis=-1, keepdims=True)
+    normed = widened * lax.rsqrt(mean_square + 1e-06)
+    low, high = normed[:, :half], normed[:, half:]
+    first = at_depth == 0
+    own_ref[...] = jnp.where(first, low, high).astype(jnp.bfloat16)
+    other_ref[...] = jnp.where(first, high, low).astype(jnp.bfloat16)
+
+
+def table_kernel(sizes, slot_hbm, blocks_hbm, place_ref, limit_ref, route_ref, *scratch):
     wide, halves, rows = sizes
+    slot_ref, blocks_ref, slot_sem, blocks_sem = scratch
+    slot_copy = pltpu.make_async_copy(slot_hbm, slot_ref, slot_sem)
+    blocks_copy = pltpu.make_async_copy(blocks_hbm, blocks_ref, blocks_sem)
+    slot_copy.start()
+    blocks_copy.start()
+    slot_copy.wait()
+    blocks_copy.wait()
     at_wide, at_depth = lax.axis_index("wide"), lax.axis_index("depth")
     total = slot_ref.shape[1]
     slots = slot_ref[...]
@@ -50,15 +69,11 @@
     pieces = len(refs) - 1 - 4 - 1
     piece_refs, weight_ref = refs[:pieces], refs[pieces]
     out_refs, rows_ref = refs[pieces + 1 : pieces + 5], refs[pieces + 5]
-    half = weight_ref.shape[0]
-    at_depth = lax.axis_index("depth")
     for k, piece in enumerate(piece_refs):
         rows_ref[k * rows : (k + 1) * rows, :] = piece[...].astype(jnp.float32)
-    widened = rows_ref[...]
-    mean_square = jnp.mean(widened * widened, axis=-1, keepdims=True)
-    used = rows_ref[:, pl.ds(pl.multiple_of(at_depth * half, LANES), half)]
-    normed = (used * lax.rsqrt(mean_square + 1e-06)).astype(jnp.bfloat16)
-    sums = jnp.dot(normed, weight_ref[...], preferred_element_type=jnp.float32)
+    sums = jnp.dot(
+        rows_ref[...].astype(jnp.bfloat16), weight_ref[...], preferred_element_type=jnp.float32
+    )
     place = place_ref[...]
     for c in range(sums.shape[1] // LANES):
         span = slice(c * LANES, (c + 1) * LANES)
@@ -120,12 +135,12 @@
     out_ref[...] = total.astype(jnp.bfloat16)
 
 
-def local_call(kernel, out_shape, count, mib, scratch=(), cost=None):
+def local_call(kernel, out_shape, count, mib, scratch=(), cost=None, spec=VMEM):
     several = isinstance(out_shape, list)
     return pl.pallas_call(
         kernel,
         out_shape=out_shape,
-        in_specs=[VMEM] * count,
+        in_specs=[spec] * count,
         out_specs=[VMEM] * len(out_shape) if several else VMEM,
         scratch_shapes=scratch,
         compiler_params=pltpu.CompilerParams(vmem_limit_bytes=mib * MIB),
@@ -133,10 +148,14 @@
     )
 
 
+def cost_of(flops):
+    return pl.CostEstimate(flops=flops, bytes_accessed=0, transcendentals=0)
+
+
 def shards(
     hidden_state, query_weight, output_weight, cache_keys, cache_values, enc_blocks, cache_slot
 ):
-    rows, model = hidden_state.shape
+    rows = hidden_state.shape[0]
     wide, narrow, halves = (lax.axis_size(name) for name in ("wide", "narrow", "depth"))
     features = query_weight.shape[1]
     cache_len = cache_keys.shape[1]
@@ -160,22 +179,31 @@
         ],
         2,
         1,
-        cost=pl.CostEstimate(flops=10**10, bytes_accessed=0, transcendentals=0),
+        scratch=[
+            pltpu.VMEM((1, cache_slot.shape[0]), jnp.int32),
+            pltpu.VMEM((1, cache_slot.shape[0]), jnp.int32),
+            pltpu.SemaphoreType.DMA(()),
+            pltpu.SemaphoreType.DMA(()),
+        ],
+        cost=cost_of(10**9),
+        spec=pl.BlockSpec(memory_space=pltpu.HBM),
     )(cache_slot[None], enc_blocks[None])
+    half_rows = shape((rows, query_weight.shape[0]), jnp.bfloat16)
+    own, other = local_call(norm_kernel, [half_rows, half_rows], 1, 1, cost=cost_of(5 * 10**9))(hidden_state)
     pieces = []
     for chip in range(wide // 2):
         for flip_depth in range(halves):
             if chip == 0 and flip_depth == 0:
-                pieces.append(hidden_state)
+                pieces.append(own)
             else:
                 flip_wide = chip * 2 + crossing(chip, flip_depth)
-                pieces.append(flipped(hidden_state, flip_wide, flip_depth))
+                pieces.append(flipped(other if flip_depth else own, flip_wide, flip_depth))
     parts = local_call(
         lambda *refs: query_kernel(rows, *refs),
         [shape((rows, features), jnp.float32)] * 4,
         len(pieces) + 2,
         6,
-        scratch=[pltpu.VMEM((len(pieces) * rows, model), jnp.float32)],
+        scratch=[pltpu.VMEM((len(pieces) * rows, query_weight.shape[0]), jnp.float32)],
     )(place, *pieces, query_weight)
     arrived = [parts[0]] + [flipped(parts[k], k // 2, k % 2) for k in range(1, 4)]
     spread = local_call(

time: 29.3 us -> 28 us (0.956)
  blocking collectives: 12.5 us -> 11.4 us
  local copies, waits for them, and re-layouts: 1.66 us -> 0.74 us
  waiting for transfers between devices: 4.92 us -> 5.36 us
    all_to_all x1, blocking collectives: 12.5 us -> 11.4 us  [shards(): gathered = lax.all_to_all(spread, ('wide', 'narrow'), 0, 0, tiled=True)]
    unnamed x16 -> x14, local copies, waits for them, and re-layouts: 1.66 us -> 0.74 us
    ppermute x6, waiting for transfers between devices: 4.92 us -> 5.36 us  [flipped(): return lax.ppermute(x, ('wide', 'depth'), pairs)]
  transfers between devices with their start and end apart: 6 -> 6, of which waited for: 3 -> 3; matrix products, arithmetic and copies ran while one was open for 0% -> 0% of each run, Pallas kernels for 0% -> 1%
where the time goes in v6:
time: 28 us; the launch traced here: 27.8 us
  blocking collectives  11.4 us (41%)
  starting transfers between devices  6.5 us (23%)
  waiting for transfers between devices  5.36 us (19%)
  Pallas kernels  3.73 us (13%)
  local copies, waits for them, and re-layouts  0.74 us (3%)
    all_to_all x1, blocking collectives, shards(): gathered = lax.all_to_all(spread, ('wide', 'narrow'), 0, 0, tiled=True)  11.4 us
    ppermute x6, starting transfers between devices, flipped(): return lax.ppermute(x, ('wide', 'depth'), pairs)  6.5 us
    ppermute x6, waiting for transfers between devices, flipped(): return lax.ppermute(x, ('wide', 'depth'), pairs)  5.36 us
    pallas_call x1, Pallas kernels, shards(): local_call(lambda *refs: attend_kernel(narrow, *refs), shape((wide * narr...  2.16 us
    unnamed x14, local copies, waits for them, and re-layouts  0.74 us
    pallas_call x1, Pallas kernels, shards(): local_call(lambda *refs: query_kernel(rows, *refs), [shape((rows, feature...  0.66 us
    pallas_call x1, Pallas kernels, shards(): local_call(sum_kernel, shape((rows, width // narrow), jnp.bfloat16), 1, 1)  0.62 us
  transfers between devices with their start and end apart: 6, of which 3 were waited for; matrix products, arithmetic and copies ran while one was open for 0% of the time, Pallas kernels for 1%

profile of v6, /device:TPU:0, one launch (start us, length us, event | category | flops | bytes accessed | tf_op | source)
XLA Modules:
  0.0 27.8 jit_solution(4378802323601946403)
XLA Ops:
  0.0 0.0 copy-start.4
  0.0 0.7 %copy-done.4 = bf16[2,4096]{1,0:T(2,128)(2,1)S(1)} copy-done((bf16[2,4096]{1,0:T(2,128)(2,1)S(1)}, bf16[2,4096]{1,0:T(2,128)(2,1)}, u32[]{:S(2)}) %copy-start.4) | copy-done | bytes 16408
  0.7 0.0 copy-start.5
  0.7 0.0 copy-start.6
  0.7 0.0 copy-start.1
  0.7 0.0 copy-start
  0.7 0.1 shard_map.74
  0.9 0.0 copy-start.2
  0.9 0.0 copy-start.3
  0.9 4.0 %collective-permute-start.2 = (bf16[2,2048]{1,0:T(2,128)(2,1)S(1)}, bf16[2,2048]{1,0:T(2,128)(2,1)S(1)}, u32[]{:S(2)}, u32[]{:S(2)}) collective-permute-start(bf16[2,2048]{1,0:T(2,128)(2,1)S(1)} %get-tuple-element.18), channel_id=1, source_target_pairs={{0,17},{1,16},{8,25},{9,24},{16,1},{17,0},{24,9},{25,8},{2,19},{3,... | collective-permute-start | bytes 24584 | tf_op jit(solution)/shard_map/ppermute | solution.py:170
  4.9 0.0 collective-permute-start
  4.9 0.4 %collective-permute-start.1 = (bf16[2,2048]{1,0:T(2,128)(2,1)S(1)}, bf16[2,2048]{1,0:T(2,128)(2,1)S(1)}, u32[]{:S(2)}, u32[]{:S(2)}) collective-permute-start(bf16[2,2048]{1,0:T(2,128)(2,1)S(1)} %get-tuple-element.17.refs_1_), channel_id=1, source_target_pairs={{0,24},{1,25},{8,16},{9,17},{16,8},{17,9},{24,0},{25,1},{2,26},{3,... | collective-permute-start | bytes 24584 | tf_op jit(solution)/shard_map/ppermute | solution.py:170
  5.3 0.0 copy-done.5
  5.3 0.0 copy-done.6
  5.3 0.1 shard_map.73
  5.4 2.6 %collective-permute-done.1.refs_3_ = bf16[2,2048]{1,0:T(2,128)(2,1)S(1)} collective-permute-done((bf16[2,2048]{1,0:T(2,128)(2,1)S(1)}, bf16[2,2048]{1,0:T(2,128)(2,1)S(1)}, u32[]{:S(2)}, u32[]{:S(2)}) %collective-permute-start.1) | collective-permute-done | bytes 8224 | tf_op jit(solution)/shard_map/ppermute | solution.py:170
  8.0 0.0 collective-permute-done.2.refs_4_
  8.0 0.0 collective-permute-done.refs_2_
  8.0 0.0 copy-done.1
  8.0 0.7 %shard_map.75 = (f32[2,1024]{1,0:T(2,128)S(1)}, f32[2,1024]{1,0:T(2,128)S(1)}, f32[2,1024]{1,0:T(2,128)S(1)}, f32[2,1024]{1,0:T(2,128)S(1)}) custom-call(s32[8,128]{1,0:T(8,128)S(1)} %get-tuple-element.16.refs_0_, bf16[2,2048]{1,0:T(2,128)(2,1)S(1)} %get-tuple-element.17.refs_1_, bf16[2,2048]{1,0:T(2,128)(2,1)S(1)} %collective-permute-done.refs_2_, ...), custom_call_target="tpu_custom_call" | custom-call | tf_op jit(solution)/shard_map/pallas_call | solution.py:201
  8.6 1.2 %collective-permute-start.3 = (f32[2,1024]{1,0:T(2,128)S(1)}, f32[2,1024]{1,0:T(2,128)S(1)}, u32[]{:S(2)}, u32[]{:S(2)}) collective-permute-start(f32[2,1024]{1,0:T(2,128)S(1)} %get-tuple-element.20), channel_id=1, source_target_pairs={{0,1},{1,0},{8,9},{9,8},{16,17},{17,16},{24,25},{25,24},{2,3},{3,2... | collective-permute-start | bytes 24584 | tf_op jit(solution)/shard_map/ppermute | solution.py:170
  9.8 0.7 %collective-permute-start.4 = (f32[2,1024]{1,0:T(2,128)S(1)}, f32[2,1024]{1,0:T(2,128)S(1)}, u32[]{:S(2)}, u32[]{:S(2)}) collective-permute-start(f32[2,1024]{1,0:T(2,128)S(1)} %get-tuple-element.21), channel_id=1, source_target_pairs={{0,8},{1,9},{8,0},{9,1},{16,24},{17,25},{24,16},{25,17},{2,10},{3,... | collective-permute-start | bytes 24584 | tf_op jit(solution)/shard_map/ppermute | solution.py:170
  10.5 0.3 %collective-permute-start.5 = (f32[2,1024]{1,0:T(2,128)S(1)}, f32[2,1024]{1,0:T(2,128)S(1)}, u32[]{:S(2)}, u32[]{:S(2)}) collective-permute-start(f32[2,1024]{1,0:T(2,128)S(1)} %get-tuple-element.22), channel_id=1, source_target_pairs={{0,9},{1,8},{8,1},{9,0},{16,25},{17,24},{24,17},{25,16},{2,11},{3,... | collective-permute-start | bytes 24584 | tf_op jit(solution)/shard_map/ppermute | solution.py:170
  10.8 1.5 %collective-permute-done.3.refs_3_ = f32[2,1024]{1,0:T(2,128)S(1)} collective-permute-done((f32[2,1024]{1,0:T(2,128)S(1)}, f32[2,1024]{1,0:T(2,128)S(1)}, u32[]{:S(2)}, u32[]{:S(2)}) %collective-permute-start.3) | collective-permute-done | bytes 8224 | tf_op jit(solution)/shard_map/ppermute | solution.py:170
  12.3 0.0 collective-permute-done.4.refs_4_
  12.3 1.3 %collective-permute-done.5.refs_5_ = f32[2,1024]{1,0:T(2,128)S(1)} collective-permute-done((f32[2,1024]{1,0:T(2,128)S(1)}, f32[2,1024]{1,0:T(2,128)S(1)}, u32[]{:S(2)}, u32[]{:S(2)}) %collective-permute-start.5) | collective-permute-done | bytes 8224 | tf_op jit(solution)/shard_map/ppermute | solution.py:170
  13.6 0.0 copy-done
  13.6 0.0 copy-done.2
  13.6 0.0 copy-done.3
  13.6 2.2 %shard_map.76 = bf16[16,2,1024]{2,1,0:T(2,128)(2,1)S(1)} custom-call(s32[2,16,512]{2,1,0:T(8,128)S(1)} %get-tuple-element.14.refs_0_, s32[8,1024]{1,0:T(8,128)S(1)} %get-tuple-element.15.refs_1_, f32[2,1024]{1,0:T(2,128)S(1)} %get-tuple-element.19.refs_2_, f32[2,1024]{1,0:T(2,128)S(1)} %collective-permute-done.3.refs_3_, ...), custom_call_target="tpu_custom_call" | custom-call | tf_op jit(solution)/shard_map/pallas_call | solution.py:209
  15.8 11.4 %all_to_all.5.parts_ref = bf16[16,2,1024]{2,1,0:T(2,128)(2,1)S(1)} all-to-all(bf16[16,2,1024]{2,1,0:T(2,128)(2,1)S(1)} %shard_map.76), channel_id=1, replica_groups=mesh['wide'=4,'narrow'=4,'depth'=2] {'wide','narrow'}, dimensions={0} | all-to-all | bytes 131072 | tf_op jit(solution)/shard_map/all_to_all | solution.py:215
  27.2 0.6 %shard_map.77 = bf16[2,1024]{1,0:T(2,128)(2,1)} custom-call(bf16[16,2,1024]{2,1,0:T(2,128)(2,1)S(1)} %all_to_all.5.parts_ref), custom_call_target="tpu_custom_call" | custom-call | tf_op jit(solution)/shard_map/pallas_call | solution.py:216
Async XLA Ops:
  0.0 0.7 %copy-start.4 = (bf16[2,4096]{1,0:T(2,128)(2,1)S(1)}, bf16[2,4096]{1,0:T(2,128)(2,1)}, u32[]{:S(2)}) copy-start(bf16[2,4096]{1,0:T(2,128)(2,1)} %hidden_ref.1) | copy-start | bytes 49156
  0.7 4.5 %copy-start.5 = (s32[16]{0:T(128)S(1)}, s32[16]{0:T(128)}, u32[]{:S(2)}) copy-start(s32[16]{0:T(128)} %param.13) | copy-start | bytes 196
  0.7 4.5 %copy-start.6 = (s32[16]{0:T(128)S(1)}, s32[16]{0:T(128)}, u32[]{:S(2)}) copy-start(s32[16]{0:T(128)} %param.12) | copy-start | bytes 196
  0.7 7.3 %copy-start.1 = (bf16[2048,1024]{1,0:T(8,128)(2,1)S(1)}, bf16[2048,1024]{1,0:T(8,128)(2,1)}, u32[]{:S(2)}) copy-start(bf16[2048,1024]{1,0:T(8,128)(2,1)} %refs_5_.1) | copy-start | bytes 12582916
  0.7 12.9 %copy-start = (bf16[1024,4096]{1,0:T(8,128)(2,1)S(1)}, bf16[1024,4096]{1,0:T(8,128)(2,1)}, u32[]{:S(2)}) copy-start(bf16[1024,4096]{1,0:T(8,128)(2,1)} %refs_8_.1) | copy-start | bytes 25165828
  0.9 12.7 %copy-start.2 = (bf16[2,512,1024]{2,1,0:T(8,128)(2,1)S(1)}, bf16[2,512,1024]{2,1,0:T(8,128)(2,1)}, u32[]{:S(2)}) copy-start(bf16[2,512,1024]{2,1,0:T(8,128)(2,1)} %refs_6_.1) | copy-start | bytes 6291460
  0.9 12.7 %copy-start.3 = (bf16[2,512,1024]{2,1,0:T(8,128)(2,1)S(1)}, bf16[2,512,1024]{2,1,0:T(8,128)(2,1)}, u32[]{:S(2)}) copy-start(bf16[2,512,1024]{2,1,0:T(8,128)(2,1)} %refs_7_.1) | copy-start | bytes 6291460
  0.9 7.1 %collective-permute-start.2 = (bf16[2,2048]{1,0:T(2,128)(2,1)S(1)}, bf16[2,2048]{1,0:T(2,128)(2,1)S(1)}, u32[]{:S(2)}, u32[]{:S(2)}) collective-permute-start(bf16[2,2048]{1,0:T(2,128)(2,1)S(1)} %get-tuple-element.18), channel_id=1, source_target_pairs={{0,17},{1,16},{8,25},{9,24},{16,1},{17,0},{24,9},{25,8},{2,19},{3,... | collective-permute-start | bytes 24584 | tf_op jit(solution)/shard_map/ppermute | solution.py:170
  4.9 3.1 %collective-permute-start = (bf16[2,2048]{1,0:T(2,128)(2,1)S(1)}, bf16[2,2048]{1,0:T(2,128)(2,1)S(1)}, u32[]{:S(2)}, u32[]{:S(2)}) collective-permute-start(bf16[2,2048]{1,0:T(2,128)(2,1)S(1)} %get-tuple-element.18), channel_id=1, source_target_pairs={{0,9},{1,8},{8,1},{9,0},{16,25},{17,24},{24,17},{25,16},{2,11},{3,... | collective-permute-start | bytes 24584 | tf_op jit(solution)/shard_map/ppermute | solution.py:170
  4.9 3.1 %collective-permute-start.1 = (bf16[2,2048]{1,0:T(2,128)(2,1)S(1)}, bf16[2,2048]{1,0:T(2,128)(2,1)S(1)}, u32[]{:S(2)}, u32[]{:S(2)}) collective-permute-start(bf16[2,2048]{1,0:T(2,128)(2,1)S(1)} %get-tuple-element.17.refs_1_), channel_id=1, source_target_pairs={{0,24},{1,25},{8,16},{9,17},{16,8},{17,9},{24,0},{25,1},{2,26},{3,... | collective-permute-start | bytes 24584 | tf_op jit(solution)/shard_map/ppermute | solution.py:170
  8.6 3.7 %collective-permute-start.3 = (f32[2,1024]{1,0:T(2,128)S(1)}, f32[2,1024]{1,0:T(2,128)S(1)}, u32[]{:S(2)}, u32[]{:S(2)}) collective-permute-start(f32[2,1024]{1,0:T(2,128)S(1)} %get-tuple-element.20), channel_id=1, source_target_pairs={{0,1},{1,0},{8,9},{9,8},{16,17},{17,16},{24,25},{25,24},{2,3},{3,2... | collective-permute-start | bytes 24584 | tf_op jit(solution)/shard_map/ppermute | solution.py:170
  9.8 2.5 %collective-permute-start.4 = (f32[2,1024]{1,0:T(2,128)S(1)}, f32[2,1024]{1,0:T(2,128)S(1)}, u32[]{:S(2)}, u32[]{:S(2)}) collective-permute-start(f32[2,1024]{1,0:T(2,128)S(1)} %get-tuple-element.21), channel_id=1, source_target_pairs={{0,8},{1,9},{8,0},{9,1},{16,24},{17,25},{24,16},{25,17},{2,10},{3,... | collective-permute-start | bytes 24584 | tf_op jit(solution)/shard_map/ppermute | solution.py:170
  10.5 3.1 %collective-permute-start.5 = (f32[2,1024]{1,0:T(2,128)S(1)}, f32[2,1024]{1,0:T(2,128)S(1)}, u32[]{:S(2)}, u32[]{:S(2)}) collective-permute-start(f32[2,1024]{1,0:T(2,128)S(1)} %get-tuple-element.22), channel_id=1, source_target_pairs={{0,9},{1,8},{8,1},{9,0},{16,25},{17,24},{24,17},{25,16},{2,11},{3,... | collective-permute-start | bytes 24584 | tf_op jit(solution)/shard_map/ppermute | solution.py:170

commit v7 on v6

--- a/solution.py
+++ b/solution.py
@@ -65,11 +65,11 @@
     route_ref[...] = jnp.broadcast_to(held - base, route_ref.shape)
 
 
-def query_kernel(rows, place_ref, *refs):
+def query_kernel(rows, order, place_ref, *refs):
     pieces = len(refs) - 1 - 4 - 1
     piece_refs, weight_ref = refs[:pieces], refs[pieces]
     out_refs, rows_ref = refs[pieces + 1 : pieces + 5], refs[pieces + 5]
-    for k, piece in enumerate(piece_refs):
+    for k, piece in zip(order, piece_refs):
         rows_ref[k * rows : (k + 1) * rows, :] = piece[...].astype(jnp.float32)
     sums = jnp.dot(
         rows_ref[...].astype(jnp.bfloat16), weight_ref[...], preferred_element_type=jnp.float32
@@ -190,22 +190,20 @@
     )(cache_slot[None], enc_blocks[None])
     half_rows = shape((rows, query_weight.shape[0]), jnp.bfloat16)
     own, other = local_call(norm_kernel, [half_rows, half_rows], 1, 1, cost=cost_of(5 * 10**9))(hidden_state)
-    pieces = []
-    for chip in range(wide // 2):
-        for flip_depth in range(halves):
-            if chip == 0 and flip_depth == 0:
-                pieces.append(own)
-            else:
-                flip_wide = chip * 2 + crossing(chip, flip_depth)
-                pieces.append(flipped(other if flip_depth else own, flip_wide, flip_depth))
+    pieces, order = [own], [0]
+    for k in range(1, wide // 2 * halves):
+        chip, flip_depth = k // halves, k % halves
+        flip_wide = chip * 2 + crossing(chip, flip_depth)
+        pieces.append(flipped(other if flip_depth else own, flip_wide, flip_depth))
+        order.append(k)
     parts = local_call(
-        lambda *refs: query_kernel(rows, *refs),
+        lambda *refs: query_kernel(rows, order, *refs),
         [shape((rows, features), jnp.float32)] * 4,
         len(pieces) + 2,
         6,
         scratch=[pltpu.VMEM((len(pieces) * rows, query_weight.shape[0]), jnp.float32)],
     )(place, *pieces, query_weight)
-    arrived = [parts[0]] + [flipped(parts[k], k // 2, k % 2) for k in range(1, 4)]
+    arrived = [parts[0]] + [flipped(parts[k], k // 2, k % 2) for k in (1, 3, 2)]
     spread = local_call(
         lambda *refs: attend_kernel(narrow, *refs),
         shape((wide * narrow, rows, width // narrow), jnp.bfloat16),

time: 28 us -> 27.7 us (0.989)
  waiting for transfers between devices: 5.36 us -> 4.68 us
  blocking collectives: 11.4 us -> 11.8 us
    ppermute x6, waiting for transfers between devices: 5.36 us -> 4.68 us  [flipped(): return lax.ppermute(x, ('wide', 'depth'), pairs)]
    all_to_all x1, blocking collectives: 11.4 us -> 11.8 us  [shards(): gathered = lax.all_to_all(spread, ('wide', 'narrow'), 0, 0, tiled=True)]
where the time goes in v7:
time: 27.7 us; the launch traced here: 27.5 us
  blocking collectives  11.8 us (43%)
  starting transfers between devices  6.5 us (23%)
  waiting for transfers between devices  4.68 us (17%)
  Pallas kernels  3.73 us (13%)
  local copies, waits for them, and re-layouts  0.74 us (3%)
    all_to_all x1, blocking collectives, shards(): gathered = lax.all_to_all(spread, ('wide', 'narrow'), 0, 0, tiled=True)  11.8 us
    ppermute x6, starting transfers between devices, flipped(): return lax.ppermute(x, ('wide', 'depth'), pairs)  6.5 us
    ppermute x6, waiting for transfers between devices, flipped(): return lax.ppermute(x, ('wide', 'depth'), pairs)  4.68 us
    pallas_call x1, Pallas kernels, shards(): local_call(lambda *refs: attend_kernel(narrow, *refs), shape((wide * narr...  2.16 us
    unnamed x14, local copies, waits for them, and re-layouts  0.74 us
    pallas_call x1, Pallas kernels, shards(): local_call(lambda *refs: query_kernel(rows, order, *refs), [shape((rows,...  0.66 us
    pallas_call x1, Pallas kernels, shards(): local_call(sum_kernel, shape((rows, width // narrow), jnp.bfloat16), 1, 1)  0.62 us
  transfers between devices with their start and end apart: 6, of which 3 were waited for; matrix products, arithmetic and copies ran while one was open for 0% of the time, Pallas kernels for 1%

profile of v7, /device:TPU:0, one launch (start us, length us, event | category | flops | bytes accessed | tf_op | source)
XLA Modules:
  0.0 27.5 jit_solution(7884390848797405543)
XLA Ops:
  0.0 0.0 copy-start.4
  0.0 0.7 %copy-done.4 = bf16[2,4096]{1,0:T(2,128)(2,1)S(1)} copy-done((bf16[2,4096]{1,0:T(2,128)(2,1)S(1)}, bf16[2,4096]{1,0:T(2,128)(2,1)}, u32[]{:S(2)}) %copy-start.4) | copy-done | bytes 16408
  0.7 0.0 copy-start.5
  0.7 0.0 copy-start.6
  0.7 0.0 copy-start.1
  0.7 0.0 copy-start
  0.7 0.1 shard_map.74
  0.9 0.0 copy-start.2
  0.9 0.0 copy-start.3
  0.9 4.0 %collective-permute-start.2 = (bf16[2,2048]{1,0:T(2,128)(2,1)S(1)}, bf16[2,2048]{1,0:T(2,128)(2,1)S(1)}, u32[]{:S(2)}, u32[]{:S(2)}) collective-permute-start(bf16[2,2048]{1,0:T(2,128)(2,1)S(1)} %get-tuple-element.18), channel_id=1, source_target_pairs={{0,17},{1,16},{8,25},{9,24},{16,1},{17,0},{24,9},{25,8},{2,19},{3,... | collective-permute-start | bytes 24584 | tf_op jit(solution)/shard_map/ppermute | solution.py:170
  4.9 0.0 collective-permute-start
  4.9 0.4 %collective-permute-start.1 = (bf16[2,2048]{1,0:T(2,128)(2,1)S(1)}, bf16[2,2048]{1,0:T(2,128)(2,1)S(1)}, u32[]{:S(2)}, u32[]{:S(2)}) collective-permute-start(bf16[2,2048]{1,0:T(2,128)(2,1)S(1)} %get-tuple-element.17.refs_1_), channel_id=1, source_target_pairs={{0,24},{1,25},{8,16},{9,17},{16,8},{17,9},{24,0},{25,1},{2,26},{3,... | collective-permute-start | bytes 24584 | tf_op jit(solution)/shard_map/ppermute | solution.py:170
  5.3 0.0 copy-done.5
  5.3 0.0 copy-done.6
  5.3 0.1 shard_map.73
  5.4 2.6 %collective-permute-done.1.refs_3_ = bf16[2,2048]{1,0:T(2,128)(2,1)S(1)} collective-permute-done((bf16[2,2048]{1,0:T(2,128)(2,1)S(1)}, bf16[2,2048]{1,0:T(2,128)(2,1)S(1)}, u32[]{:S(2)}, u32[]{:S(2)}) %collective-permute-start.1) | collective-permute-done | bytes 8224 | tf_op jit(solution)/shard_map/ppermute | solution.py:170
  8.0 0.0 collective-permute-done.2.refs_4_
  8.0 0.0 collective-permute-done.refs_2_
  8.0 0.0 copy-done.1
  8.0 0.7 %shard_map.75 = (f32[2,1024]{1,0:T(2,128)S(1)}, f32[2,1024]{1,0:T(2,128)S(1)}, f32[2,1024]{1,0:T(2,128)S(1)}, f32[2,1024]{1,0:T(2,128)S(1)}) custom-call(s32[8,128]{1,0:T(8,128)S(1)} %get-tuple-element.16.refs_0_, bf16[2,2048]{1,0:T(2,128)(2,1)S(1)} %get-tuple-element.17.refs_1_, bf16[2,2048]{1,0:T(2,128)(2,1)S(1)} %collective-permute-done.refs_2_, ...), custom_call_target="tpu_custom_call" | custom-call | tf_op jit(solution)/shard_map/pallas_call | solution.py:199
  8.6 1.2 %collective-permute-start.3 = (f32[2,1024]{1,0:T(2,128)S(1)}, f32[2,1024]{1,0:T(2,128)S(1)}, u32[]{:S(2)}, u32[]{:S(2)}) collective-permute-start(f32[2,1024]{1,0:T(2,128)S(1)} %get-tuple-element.20), channel_id=1, source_target_pairs={{0,1},{1,0},{8,9},{9,8},{16,17},{17,16},{24,25},{25,24},{2,3},{3,2... | collective-permute-start | bytes 24584 | tf_op jit(solution)/shard_map/ppermute | solution.py:170
  9.8 0.8 %collective-permute-start.4 = (f32[2,1024]{1,0:T(2,128)S(1)}, f32[2,1024]{1,0:T(2,128)S(1)}, u32[]{:S(2)}, u32[]{:S(2)}) collective-permute-start(f32[2,1024]{1,0:T(2,128)S(1)} %get-tuple-element.21), channel_id=1, source_target_pairs={{0,9},{1,8},{8,1},{9,0},{16,25},{17,24},{24,17},{25,16},{2,11},{3,... | collective-permute-start | bytes 24584 | tf_op jit(solution)/shard_map/ppermute | solution.py:170
  10.7 0.1 collective-permute-start.5
  10.8 1.5 %collective-permute-done.3.refs_3_ = f32[2,1024]{1,0:T(2,128)S(1)} collective-permute-done((f32[2,1024]{1,0:T(2,128)S(1)}, f32[2,1024]{1,0:T(2,128)S(1)}, u32[]{:S(2)}, u32[]{:S(2)}) %collective-permute-start.3) | collective-permute-done | bytes 8224 | tf_op jit(solution)/shard_map/ppermute | solution.py:170
  12.3 0.6 %collective-permute-done.4.refs_4_ = f32[2,1024]{1,0:T(2,128)S(1)} collective-permute-done((f32[2,1024]{1,0:T(2,128)S(1)}, f32[2,1024]{1,0:T(2,128)S(1)}, u32[]{:S(2)}, u32[]{:S(2)}) %collective-permute-start.4) | collective-permute-done | bytes 8224 | tf_op jit(solution)/shard_map/ppermute | solution.py:170
  12.9 0.0 collective-permute-done.5.refs_5_
  12.9 0.0 copy-done
  12.9 0.0 copy-done.2
  12.9 0.0 copy-done.3
  12.9 2.2 %shard_map.76 = bf16[16,2,1024]{2,1,0:T(2,128)(2,1)S(1)} custom-call(s32[2,16,512]{2,1,0:T(8,128)S(1)} %get-tuple-element.14.refs_0_, s32[8,1024]{1,0:T(8,128)S(1)} %get-tuple-element.15.refs_1_, f32[2,1024]{1,0:T(2,128)S(1)} %get-tuple-element.19.refs_2_, f32[2,1024]{1,0:T(2,128)S(1)} %collective-permute-done.3.refs_3_, ...), custom_call_target="tpu_custom_call" | custom-call | tf_op jit(solution)/shard_map/pallas_call | solution.py:207
  15.1 11.8 %all_to_all.5.parts_ref = bf16[16,2,1024]{2,1,0:T(2,128)(2,1)S(1)} all-to-all(bf16[16,2,1024]{2,1,0:T(2,128)(2,1)S(1)} %shard_map.76), channel_id=1, replica_groups=mesh['wide'=4,'narrow'=4,'depth'=2] {'wide','narrow'}, dimensions={0} | all-to-all | bytes 131072 | tf_op jit(solution)/shard_map/all_to_all | solution.py:213
  26.9 0.6 %shard_map.77 = bf16[2,1024]{1,0:T(2,128)(2,1)} custom-call(bf16[16,2,1024]{2,1,0:T(2,128)(2,1)S(1)} %all_to_all.5.parts_ref), custom_call_target="tpu_custom_call" | custom-call | tf_op jit(solution)/shard_map/pallas_call | solution.py:214
Async XLA Ops:
  0.0 0.7 %copy-start.4 = (bf16[2,4096]{1,0:T(2,128)(2,1)S(1)}, bf16[2,4096]{1,0:T(2,128)(2,1)}, u32[]{:S(2)}) copy-start(bf16[2,4096]{1,0:T(2,128)(2,1)} %hidden_ref.1) | copy-start | bytes 49156
  0.7 4.5 %copy-start.5 = (s32[16]{0:T(128)S(1)}, s32[16]{0:T(128)}, u32[]{:S(2)}) copy-start(s32[16]{0:T(128)} %param.13) | copy-start | bytes 196
  0.7 4.5 %copy-start.6 = (s32[16]{0:T(128)S(1)}, s32[16]{0:T(128)}, u32[]{:S(2)}) copy-start(s32[16]{0:T(128)} %param.12) | copy-start | bytes 196
  0.7 7.3 %copy-start.1 = (bf16[2048,1024]{1,0:T(8,128)(2,1)S(1)}, bf16[2048,1024]{1,0:T(8,128)(2,1)}, u32[]{:S(2)}) copy-start(bf16[2048,1024]{1,0:T(8,128)(2,1)} %refs_5_.1) | copy-start | bytes 12582916
  0.7 12.2 %copy-start = (bf16[1024,4096]{1,0:T(8,128)(2,1)S(1)}, bf16[1024,4096]{1,0:T(8,128)(2,1)}, u32[]{:S(2)}) copy-start(bf16[1024,4096]{1,0:T(8,128)(2,1)} %refs_8_.1) | copy-start | bytes 25165828
  0.9 12.0 %copy-start.2 = (bf16[2,512,1024]{2,1,0:T(8,128)(2,1)S(1)}, bf16[2,512,1024]{2,1,0:T(8,128)(2,1)}, u32[]{:S(2)}) copy-start(bf16[2,512,1024]{2,1,0:T(8,128)(2,1)} %refs_6_.1) | copy-start | bytes 6291460
  0.9 12.0 %copy-start.3 = (bf16[2,512,1024]{2,1,0:T(8,128)(2,1)S(1)}, bf16[2,512,1024]{2,1,0:T(8,128)(2,1)}, u32[]{:S(2)}) copy-start(bf16[2,512,1024]{2,1,0:T(8,128)(2,1)} %refs_7_.1) | copy-start | bytes 6291460
  0.9 7.1 %collective-permute-start.2 = (bf16[2,2048]{1,0:T(2,128)(2,1)S(1)}, bf16[2,2048]{1,0:T(2,128)(2,1)S(1)}, u32[]{:S(2)}, u32[]{:S(2)}) collective-permute-start(bf16[2,2048]{1,0:T(2,128)(2,1)S(1)} %get-tuple-element.18), channel_id=1, source_target_pairs={{0,17},{1,16},{8,25},{9,24},{16,1},{17,0},{24,9},{25,8},{2,19},{3,... | collective-permute-start | bytes 24584 | tf_op jit(solution)/shard_map/ppermute | solution.py:170
  4.9 3.1 %collective-permute-start = (bf16[2,2048]{1,0:T(2,128)(2,1)S(1)}, bf16[2,2048]{1,0:T(2,128)(2,1)S(1)}, u32[]{:S(2)}, u32[]{:S(2)}) collective-permute-start(bf16[2,2048]{1,0:T(2,128)(2,1)S(1)} %get-tuple-element.18), channel_id=1, source_target_pairs={{0,9},{1,8},{8,1},{9,0},{16,25},{17,24},{24,17},{25,16},{2,11},{3,... | collective-permute-start | bytes 24584 | tf_op jit(solution)/shard_map/ppermute | solution.py:170
  4.9 3.1 %collective-permute-start.1 = (bf16[2,2048]{1,0:T(2,128)(2,1)S(1)}, bf16[2,2048]{1,0:T(2,128)(2,1)S(1)}, u32[]{:S(2)}, u32[]{:S(2)}) collective-permute-start(bf16[2,2048]{1,0:T(2,128)(2,1)S(1)} %get-tuple-element.17.refs_1_), channel_id=1, source_target_pairs={{0,24},{1,25},{8,16},{9,17},{16,8},{17,9},{24,0},{25,1},{2,26},{3,... | collective-permute-start | bytes 24584 | tf_op jit(solution)/shard_map/ppermute | solution.py:170
  8.6 3.7 %collective-permute-start.3 = (f32[2,1024]{1,0:T(2,128)S(1)}, f32[2,1024]{1,0:T(2,128)S(1)}, u32[]{:S(2)}, u32[]{:S(2)}) collective-permute-start(f32[2,1024]{1,0:T(2,128)S(1)} %get-tuple-element.20), channel_id=1, source_target_pairs={{0,1},{1,0},{8,9},{9,8},{16,17},{17,16},{24,25},{25,24},{2,3},{3,2... | collective-permute-start | bytes 24584 | tf_op jit(solution)/shard_map/ppermute | solution.py:170
  9.8 3.1 %collective-permute-start.4 = (f32[2,1024]{1,0:T(2,128)S(1)}, f32[2,1024]{1,0:T(2,128)S(1)}, u32[]{:S(2)}, u32[]{:S(2)}) collective-permute-start(f32[2,1024]{1,0:T(2,128)S(1)} %get-tuple-element.21), channel_id=1, source_target_pairs={{0,9},{1,8},{8,1},{9,0},{16,25},{17,24},{24,17},{25,16},{2,11},{3,... | collective-permute-start | bytes 24584 | tf_op jit(solution)/shard_map/ppermute | solution.py:170
  10.7 2.3 %collective-permute-start.5 = (f32[2,1024]{1,0:T(2,128)S(1)}, f32[2,1024]{1,0:T(2,128)S(1)}, u32[]{:S(2)}, u32[]{:S(2)}) collective-permute-start(f32[2,1024]{1,0:T(2,128)S(1)} %get-tuple-element.22), channel_id=1, source_target_pairs={{0,8},{1,9},{8,0},{9,1},{16,24},{17,25},{24,16},{25,17},{2,10},{3,... | collective-permute-start | bytes 24584 | tf_op jit(solution)/shard_map/ppermute | solution.py:170

commit v8 on v7

--- a/solution.py
+++ b/solution.py
@@ -65,6 +65,11 @@
     route_ref[...] = jnp.broadcast_to(held - base, route_ref.shape)
 
 
+def turn_kernel(keys_ref, turned_ref):
+    for j in range(keys_ref.shape[0]):
+        turned_ref[j] = keys_ref[j].T
+
+
 def query_kernel(rows, order, place_ref, *refs):
     pieces = len(refs) - 1 - 4 - 1
     piece_refs, weight_ref = refs[:pieces], refs[pieces]
@@ -88,7 +93,7 @@
 
 def attend_kernel(narrow, limit_ref, route_ref, *refs):
     parts, (keys_ref, values_ref, weight_ref, out_ref) = refs[:4], refs[4:]
-    rows, cache_len, features = keys_ref.shape
+    rows, features, cache_len = keys_ref.shape
     heads = features // HDIM
     queries = (parts[0][...] + parts[2][...]) + (parts[1][...] + parts[3][...])
     of_head = (
@@ -100,9 +105,7 @@
     for j in range(rows):
         spread = jnp.where(of_head, queries[j : j + 1, :], 0.0).astype(jnp.bfloat16)
         scores.append(
-            lax.dot_general(
-                spread, keys_ref[j], (((1,), (1,)), ((), ())), preferred_element_type=jnp.float32
-            )
+            jnp.dot(spread, keys_ref[j], preferred_element_type=jnp.float32)
         )
     for j in range(rows):
         masked = jnp.where(positions < limit_ref[j], scores[j], jnp.float32(-1e30))
@@ -190,6 +193,12 @@
     )(cache_slot[None], enc_blocks[None])
     half_rows = shape((rows, query_weight.shape[0]), jnp.bfloat16)
     own, other = local_call(norm_kernel, [half_rows, half_rows], 1, 1, cost=cost_of(5 * 10**9))(hidden_state)
+    turned = local_call(
+        turn_kernel,
+        shape((rows, features, cache_len), jnp.bfloat16),
+        1,
+        6,
+    )(cache_keys)
     pieces, order = [own], [0]
     for k in range(1, wide // 2 * halves):
         chip, flip_depth = k // halves, k % halves
@@ -209,7 +218,7 @@
         shape((wide * narrow, rows, width // narrow), jnp.bfloat16),
         9,
         16,
-    )(limit, route, *arrived, cache_keys, cache_values, output_weight)
+    )(limit, route, *arrived, turned, cache_values, output_weight)
     gathered = lax.all_to_all(spread, ("wide", "narrow"), 0, 0, tiled=True)
     return local_call(
         sum_kernel, shape((rows, width // narrow), jnp.bfloat16), 1, 1

time: 27.7 us -> 27.4 us (0.989)
  waiting for transfers between devices: 4.68 us -> 4.08 us
  Pallas kernels: 3.73 us -> 4.05 us
    ppermute x6, waiting for transfers between devices: 4.68 us -> 4.08 us  [flipped(): return lax.ppermute(x, ('wide', 'depth'), pairs)]
    pallas_call x0 -> x1, Pallas kernels: none -> 0.59 us  [shards(): local_call(turn_kernel, shape((rows, features, cache_len), jnp.bfloat16),...]
  transfers between devices with their start and end apart: 6 -> 6, of which waited for: 3 -> 3; matrix products, arithmetic and copies ran while one was open for 0% -> 0% of each run, Pallas kernels for 1% -> 3%
where the time goes in v8:
time: 27.4 us; the launch traced here: 27.2 us
  blocking collectives  11.8 us (43%)
  starting transfers between devices  6.5 us (24%)
  waiting for transfers between devices  4.08 us (15%)
  Pallas kernels  4.05 us (15%)
  local copies, waits for them, and re-layouts  0.74 us (3%)
    all_to_all x1, blocking collectives, shards(): gathered = lax.all_to_all(spread, ('wide', 'narrow'), 0, 0, tiled=True)  11.8 us
    ppermute x6, starting transfers between devices, flipped(): return lax.ppermute(x, ('wide', 'depth'), pairs)  6.5 us
    ppermute x6, waiting for transfers between devices, flipped(): return lax.ppermute(x, ('wide', 'depth'), pairs)  4.08 us
    pallas_call x1, Pallas kernels, shards(): local_call(lambda *refs: attend_kernel(narrow, *refs), shape((wide * narr...  1.89 us
    unnamed x14, local copies, waits for them, and re-layouts  0.74 us
    pallas_call x1, Pallas kernels, shards(): local_call(lambda *refs: query_kernel(rows, order, *refs), [shape((rows,...  0.66 us
    pallas_call x1, Pallas kernels, shards(): local_call(sum_kernel, shape((rows, width // narrow), jnp.bfloat16), 1, 1)  0.62 us
    pallas_call x1, Pallas kernels, shards(): local_call(turn_kernel, shape((rows, features, cache_len), jnp.bfloat16),...  0.59 us
  transfers between devices with their start and end apart: 6, of which 3 were waited for; matrix products, arithmetic and copies ran while one was open for 0% of the time, Pallas kernels for 3%

profile of v8, /device:TPU:0, one launch (start us, length us, event | category | flops | bytes accessed | tf_op | source)
XLA Modules:
  0.0 27.2 jit_solution(5111039418054508841)
XLA Ops:
  0.0 0.0 copy-start.4
  0.0 0.7 %copy-done.4 = bf16[2,4096]{1,0:T(2,128)(2,1)S(1)} copy-done((bf16[2,4096]{1,0:T(2,128)(2,1)S(1)}, bf16[2,4096]{1,0:T(2,128)(2,1)}, u32[]{:S(2)}) %copy-start.4) | copy-done | bytes 16408
  0.7 0.0 copy-start.5
  0.7 0.0 copy-start.6
  0.7 0.0 copy-start.1
  0.7 0.0 copy-start.3
  0.7 0.1 shard_map.74
  0.9 4.0 %collective-permute-start.2 = (bf16[2,2048]{1,0:T(2,128)(2,1)S(1)}, bf16[2,2048]{1,0:T(2,128)(2,1)S(1)}, u32[]{:S(2)}, u32[]{:S(2)}) collective-permute-start(bf16[2,2048]{1,0:T(2,128)(2,1)S(1)} %get-tuple-element.18), channel_id=1, source_target_pairs={{0,17},{1,16},{8,25},{9,24},{16,1},{17,0},{24,9},{25,8},{2,19},{3,... | collective-permute-start | bytes 24584 | tf_op jit(solution)/shard_map/ppermute | solution.py:173
  4.9 0.0 collective-permute-start
  4.9 0.4 %collective-permute-start.1 = (bf16[2,2048]{1,0:T(2,128)(2,1)S(1)}, bf16[2,2048]{1,0:T(2,128)(2,1)S(1)}, u32[]{:S(2)}, u32[]{:S(2)}) collective-permute-start(bf16[2,2048]{1,0:T(2,128)(2,1)S(1)} %get-tuple-element.17.refs_1_), channel_id=1, source_target_pairs={{0,24},{1,25},{8,16},{9,17},{16,8},{17,9},{24,0},{25,1},{2,26},{3,... | collective-permute-start | bytes 24584 | tf_op jit(solution)/shard_map/ppermute | solution.py:173
  5.2 0.0 copy-done.5
  5.2 0.0 copy-done.6
  5.2 0.1 shard_map.73
  5.4 2.6 %collective-permute-done.1.refs_3_ = bf16[2,2048]{1,0:T(2,128)(2,1)S(1)} collective-permute-done((bf16[2,2048]{1,0:T(2,128)(2,1)S(1)}, bf16[2,2048]{1,0:T(2,128)(2,1)S(1)}, u32[]{:S(2)}, u32[]{:S(2)}) %collective-permute-start.1) | collective-permute-done | bytes 8224 | tf_op jit(solution)/shard_map/ppermute | solution.py:173
  7.9 0.0 collective-permute-done.2.refs_4_
  7.9 0.0 collective-permute-done.refs_2_
  8.0 0.0 copy-done.1
  8.0 0.0 copy-start
  8.0 0.7 %shard_map.75 = (f32[2,1024]{1,0:T(2,128)S(1)}, f32[2,1024]{1,0:T(2,128)S(1)}, f32[2,1024]{1,0:T(2,128)S(1)}, f32[2,1024]{1,0:T(2,128)S(1)}) custom-call(s32[8,128]{1,0:T(8,128)S(1)} %get-tuple-element.16.refs_0_, bf16[2,2048]{1,0:T(2,128)(2,1)S(1)} %get-tuple-element.17.refs_1_, bf16[2,2048]{1,0:T(2,128)(2,1)S(1)} %collective-permute-done.refs_2_, ...), custom_call_target="tpu_custom_call" | custom-call | tf_op jit(solution)/shard_map/pallas_call | solution.py:208
  8.6 1.2 %collective-permute-start.3 = (f32[2,1024]{1,0:T(2,128)S(1)}, f32[2,1024]{1,0:T(2,128)S(1)}, u32[]{:S(2)}, u32[]{:S(2)}) collective-permute-start(f32[2,1024]{1,0:T(2,128)S(1)} %get-tuple-element.20), channel_id=1, source_target_pairs={{0,1},{1,0},{8,9},{9,8},{16,17},{17,16},{24,25},{25,24},{2,3},{3,2... | collective-permute-start | bytes 24584 | tf_op jit(solution)/shard_map/ppermute | solution.py:173
  9.8 0.8 %collective-permute-start.4 = (f32[2,1024]{1,0:T(2,128)S(1)}, f32[2,1024]{1,0:T(2,128)S(1)}, u32[]{:S(2)}, u32[]{:S(2)}) collective-permute-start(f32[2,1024]{1,0:T(2,128)S(1)} %get-tuple-element.21), channel_id=1, source_target_pairs={{0,9},{1,8},{8,1},{9,0},{16,25},{17,24},{24,17},{25,16},{2,11},{3,... | collective-permute-start | bytes 24584 | tf_op jit(solution)/shard_map/ppermute | solution.py:173
  10.6 0.1 collective-permute-start.5
  10.8 0.0 copy-done.3
  10.8 0.6 %shard_map.76.refs_6_ = bf16[2,1024,512]{2,1,0:T(8,128)(2,1)S(1)} custom-call(bf16[2,512,1024]{2,1,0:T(8,128)(2,1)S(1)} %copy-done.3), custom_call_target="tpu_custom_call" | custom-call | tf_op jit(solution)/shard_map/pallas_call | solution.py:196
  11.4 0.9 %collective-permute-done.3.refs_3_ = f32[2,1024]{1,0:T(2,128)S(1)} collective-permute-done((f32[2,1024]{1,0:T(2,128)S(1)}, f32[2,1024]{1,0:T(2,128)S(1)}, u32[]{:S(2)}, u32[]{:S(2)}) %collective-permute-start.3) | collective-permute-done | bytes 8224 | tf_op jit(solution)/shard_map/ppermute | solution.py:173
  12.3 0.6 %collective-permute-done.4.refs_4_ = f32[2,1024]{1,0:T(2,128)S(1)} collective-permute-done((f32[2,1024]{1,0:T(2,128)S(1)}, f32[2,1024]{1,0:T(2,128)S(1)}, u32[]{:S(2)}, u32[]{:S(2)}) %collective-permute-start.4) | collective-permute-done | bytes 8224 | tf_op jit(solution)/shard_map/ppermute | solution.py:173
  12.9 0.0 collective-permute-done.5.refs_5_
  12.9 0.0 copy-done.2
  12.9 0.0 copy-done
  12.9 1.9 %shard_map.77 = bf16[16,2,1024]{2,1,0:T(2,128)(2,1)S(1)} custom-call(s32[2,16,512]{2,1,0:T(8,128)S(1)} %get-tuple-element.14.refs_0_, s32[8,1024]{1,0:T(8,128)S(1)} %get-tuple-element.15.refs_1_, f32[2,1024]{1,0:T(2,128)S(1)} %get-tuple-element.19.refs_2_, f32[2,1024]{1,0:T(2,128)S(1)} %collective-permute-done.3.refs_3_, ...), custom_call_target="tpu_custom_call" | custom-call | tf_op jit(solution)/shard_map/pallas_call | solution.py:216
  14.8 11.8 %all_to_all.5.parts_ref = bf16[16,2,1024]{2,1,0:T(2,128)(2,1)S(1)} all-to-all(bf16[16,2,1024]{2,1,0:T(2,128)(2,1)S(1)} %shard_map.77), channel_id=1, replica_groups=mesh['wide'=4,'narrow'=4,'depth'=2] {'wide','narrow'}, dimensions={0} | all-to-all | bytes 131072 | tf_op jit(solution)/shard_map/all_to_all | solution.py:222
  26.6 0.6 %shard_map.78 = bf16[2,1024]{1,0:T(2,128)(2,1)} custom-call(bf16[16,2,1024]{2,1,0:T(2,128)(2,1)S(1)} %all_to_all.5.parts_ref), custom_call_target="tpu_custom_call" | custom-call | tf_op jit(solution)/shard_map/pallas_call | solution.py:223
  (1 shorter events, 0.0 us)
Async XLA Ops:
  0.0 0.7 %copy-start.4 = (bf16[2,4096]{1,0:T(2,128)(2,1)S(1)}, bf16[2,4096]{1,0:T(2,128)(2,1)}, u32[]{:S(2)}) copy-start(bf16[2,4096]{1,0:T(2,128)(2,1)} %hidden_ref.1) | copy-start | bytes 49156
  0.7 4.5 %copy-start.5 = (s32[16]{0:T(128)S(1)}, s32[16]{0:T(128)}, u32[]{:S(2)}) copy-start(s32[16]{0:T(128)} %param.13) | copy-start | bytes 196
  0.7 4.5 %copy-start.6 = (s32[16]{0:T(128)S(1)}, s32[16]{0:T(128)}, u32[]{:S(2)}) copy-start(s32[16]{0:T(128)} %param.12) | copy-start | bytes 196
  0.7 7.2 %copy-start.1 = (bf16[2048,1024]{1,0:T(8,128)(2,1)S(1)}, bf16[2048,1024]{1,0:T(8,128)(2,1)}, u32[]{:S(2)}) copy-start(bf16[2048,1024]{1,0:T(8,128)(2,1)} %refs_5_.1) | copy-start | bytes 12582916
  0.7 10.1 %copy-start.3 = (bf16[2,512,1024]{2,1,0:T(8,128)(2,1)S(1)}, bf16[2,512,1024]{2,1,0:T(8,128)(2,1)}, u32[]{:S(2)}) copy-start(bf16[2,512,1024]{2,1,0:T(8,128)(2,1)} %keys_ref.1) | copy-start | bytes 6291460
  0.9 7.1 %collective-permute-start.2 = (bf16[2,2048]{1,0:T(2,128)(2,1)S(1)}, bf16[2,2048]{1,0:T(2,128)(2,1)S(1)}, u32[]{:S(2)}, u32[]{:S(2)}) collective-permute-start(bf16[2,2048]{1,0:T(2,128)(2,1)S(1)} %get-tuple-element.18), channel_id=1, source_target_pairs={{0,17},{1,16},{8,25},{9,24},{16,1},{17,0},{24,9},{25,8},{2,19},{3,... | collective-permute-start | bytes 24584 | tf_op jit(solution)/shard_map/ppermute | solution.py:173
  4.9 3.1 %collective-permute-start = (bf16[2,2048]{1,0:T(2,128)(2,1)S(1)}, bf16[2,2048]{1,0:T(2,128)(2,1)S(1)}, u32[]{:S(2)}, u32[]{:S(2)}) collective-permute-start(bf16[2,2048]{1,0:T(2,128)(2,1)S(1)} %get-tuple-element.18), channel_id=1, source_target_pairs={{0,9},{1,8},{8,1},{9,0},{16,25},{17,24},{24,17},{25,16},{2,11},{3,... | collective-permute-start | bytes 24584 | tf_op jit(solution)/shard_map/ppermute | solution.py:173
  4.9 3.1 %collective-permute-start.1 = (bf16[2,2048]{1,0:T(2,128)(2,1)S(1)}, bf16[2,2048]{1,0:T(2,128)(2,1)S(1)}, u32[]{:S(2)}, u32[]{:S(2)}) collective-permute-start(bf16[2,2048]{1,0:T(2,128)(2,1)S(1)} %get-tuple-element.17.refs_1_), channel_id=1, source_target_pairs={{0,24},{1,25},{8,16},{9,17},{16,8},{17,9},{24,0},{25,1},{2,26},{3,... | collective-permute-start | bytes 24584 | tf_op jit(solution)/shard_map/ppermute | solution.py:173
  5.2 7.7 %copy-start.2 = (bf16[2,512,1024]{2,1,0:T(8,128)(2,1)S(1)}, bf16[2,512,1024]{2,1,0:T(8,128)(2,1)}, u32[]{:S(2)}) copy-start(bf16[2,512,1024]{2,1,0:T(8,128)(2,1)} %refs_7_.1) | copy-start | bytes 6291460
  8.0 5.0 %copy-start = (bf16[1024,4096]{1,0:T(8,128)(2,1)S(1)}, bf16[1024,4096]{1,0:T(8,128)(2,1)}, u32[]{:S(2)}) copy-start(bf16[1024,4096]{1,0:T(8,128)(2,1)} %refs_8_.1) | copy-start | bytes 25165828
  8.6 3.7 %collective-permute-start.3 = (f32[2,1024]{1,0:T(2,128)S(1)}, f32[2,1024]{1,0:T(2,128)S(1)}, u32[]{:S(2)}, u32[]{:S(2)}) collective-permute-start(f32[2,1024]{1,0:T(2,128)S(1)} %get-tuple-element.20), channel_id=1, source_target_pairs={{0,1},{1,0},{8,9},{9,8},{16,17},{17,16},{24,25},{25,24},{2,3},{3,2... | collective-permute-start | bytes 24584 | tf_op jit(solution)/shard_map/ppermute | solution.py:173
  9.8 3.1 %collective-permute-start.4 = (f32[2,1024]{1,0:T(2,128)S(1)}, f32[2,1024]{1,0:T(2,128)S(1)}, u32[]{:S(2)}, u32[]{:S(2)}) collective-permute-start(f32[2,1024]{1,0:T(2,128)S(1)} %get-tuple-element.21), channel_id=1, source_target_pairs={{0,9},{1,8},{8,1},{9,0},{16,25},{17,24},{24,17},{25,16},{2,11},{3,... | collective-permute-start | bytes 24584 | tf_op jit(solution)/shard_map/ppermute | solution.py:173
  10.6 2.3 %collective-permute-start.5 = (f32[2,1024]{1,0:T(2,128)S(1)}, f32[2,1024]{1,0:T(2,128)S(1)}, u32[]{:S(2)}, u32[]{:S(2)}) collective-permute-start(f32[2,1024]{1,0:T(2,128)S(1)} %get-tuple-element.22), channel_id=1, source_target_pairs={{0,8},{1,9},{8,0},{9,1},{16,24},{17,25},{24,16},{25,17},{2,10},{3,... | collective-permute-start | bytes 24584 | tf_op jit(solution)/shard_map/ppermute | solution.py:173
